TPU v7x, 1024 devices: a whole 4x4x32 slice. The times are simulated.
1024 devices in a mesh: patch: 2 (over core), theta: 32 (over z), phi: 16 (over x, y).
Axes of the slice: x: 4, y: 4, z: 32, core: 2. Of those that a mesh axis runs over, the one named last changes fastest.
Arguments:
- density: float32 [2, 16, 512, 2048], P('patch', None, 'theta', 'phi'), may hold values from 0.5 to 2
- velocity: float32 [2, 3, 16, 512, 2048], P('patch', None, None, 'theta', 'phi'), may hold values from -3 to 3
- magnetic: float32 [2, 3, 16, 512, 2048], P('patch', None, None, 'theta', 'phi'), may hold values from -3 to 3
- pressure: float32 [2, 16, 512, 2048], P('patch', None, 'theta', 'phi'), may hold values from 0.5 to 2
- send_row: int32 [2, 32, 16, 96], P('patch', 'theta', 'phi'), may hold values from 0 to 14
- send_col: int32 [2, 32, 16, 96], P('patch', 'theta', 'phi'), may hold values from 0 to 126
- send_weight: float32 [2, 32, 16, 2, 96], P('patch', 'theta', 'phi'), may hold values from 0 to 1
- send_turn: float32 [2, 32, 16, 96], P('patch', 'theta', 'phi'), may hold values from -3.140625 to 3.140625
- send_dest: int32 [2, 32, 16, 96], P('patch', 'theta', 'phi'), may hold values from 0 to 5120, as said below
Outputs:
- new_density: float32 [2, 16, 512, 2048], P('patch', None, 'theta', 'phi')
- new_velocity: float32 [2, 3, 16, 512, 2048], P('patch', None, None, 'theta', 'phi')
- new_magnetic: float32 [2, 3, 16, 512, 2048], P('patch', None, None, 'theta', 'phi')
- new_pressure: float32 [2, 16, 512, 2048], P('patch', None, 'theta', 'phi')
Inputs may be any that keep to these rules, and one draw needn't show every extreme that they name: `send_dest`: each ghost point m < 5120 of a patch is named by exactly one slot of the other patch's tiles; unused slots hold 5120. Used slots lie only in tiles of the first and last tile rows and tile columns of a patch, and their donor cells lie within min(16, 128) cells of the patch's outer edge; the four corner tiles use all 96 slots, every other tile fewer.
All inputs are finite; a program needn't handle non-finite values.
Results may differ from a plain program's by a relative error of at most 0.00008.
Values sent between devices are 32-bit elements; how exact they have to be, the bound alone decides.
A program may use at most 32 MiB of HBM per device.

v0:
```python
import math

import jax
import jax.numpy as jnp
from jax import lax
from jax.sharding import Mesh
from jax.sharding import PartitionSpec as P

PHI = ("phi_0", "phi_1")
PATCH_PHI = ("patch", "phi_0", "phi_1")


GAMMA = 5.0 / 3.0
R_BASE = 0.6
DR_STEP = 0.65 / 64.0
COURANT = 0.4
DIFFUSE = 0.4


def whole_of(value, axes, dim):
    out = value
    for number in range(len(axes) - 1, -1, -1):
        out = lax.all_gather(out, axes[number], axis=dim, tiled=True)
    return out


def in_order(pieces, dim):
    shape = list(pieces.shape[1:])
    shape[dim] *= pieces.shape[0]
    return jnp.moveaxis(pieces, 0, dim).reshape(shape)


def sent_to_all(value, axis):
    copies = jnp.broadcast_to(value, (lax.axis_size(axis), *value.shape))
    return lax.all_to_all(copies, axis, split_axis=0, concat_axis=0, tiled=True)


def gathered_copies(value, axis, dim):
    return in_order(sent_to_all(value, axis), dim)


def split_up(value, dim, length):
    before, after = (value.shape[:dim], value.shape[dim + 1 :])
    return jnp.moveaxis(value.reshape(*before, length, -1, *after), dim, 0)


def sum_at_owner(value, axis, dim):
    pieces = split_up(value, dim, lax.axis_size(axis))
    arrived = lax.all_to_all(pieces, axis, split_axis=0, concat_axis=0, tiled=True)
    return arrived.sum(axis=0)


def by_axis(value, axes):
    for axis in axes:
        value = lax.psum(value, axis)
    return value


def over_copies(value, axis):
    return sent_to_all(value, axis).sum(axis=0)


def extended(value, sides, width):
    edges = {}
    for axis, dim in sides:
        size, length = (lax.axis_size(axis), value.shape[dim])
        up = [(i, (i + 1) % size) for i in range(size - 1)]
        last = lax.slice_in_dim(value, length - width, length, axis=dim)
        initial = lax.slice_in_dim(value, 0, width, axis=dim)
        edges[dim] = (
            lax.ppermute(last, axis, up),
            lax.ppermute(initial, axis, [(b, a) for a, b in up]),
        )
    done = []
    for _, dim in sides:
        low, high = edges[dim]
        around = [(width, width) if d in done else (0, 0) for d in range(value.ndim)]
        value = jnp.concatenate([jnp.pad(low, around), value, jnp.pad(high, around)], axis=dim)
        done.append(dim)
    return value


def grid_constants(total_theta, total_phi):
    d_theta = 0.5 * math.pi / total_theta
    d_phi = 1.5 * math.pi / total_phi
    r_low = R_BASE + 0.5 * DR_STEP
    inv_r = 1.0 / DR_STEP
    inv_t = 1.0 / (r_low * d_theta)
    inv_p = 1.0 / (r_low * math.sin(0.25 * math.pi) * d_phi)
    dt_step = COURANT / (inv_r + inv_t + inv_p)
    diffusivity = DIFFUSE / (dt_step * (inv_r * inv_r + inv_t * inv_t + inv_p * inv_p))
    return (d_theta, d_phi, dt_step, diffusivity)


def bilinear(low_low, low_high, high_low, high_high, weight_row, weight_col):
    return (1.0 - weight_row) * (
        (1.0 - weight_col) * low_low + weight_col * low_high
    ) + weight_row * ((1.0 - weight_col) * high_low + weight_col * high_high)


def turn_frame(blended, turn):
    cos_t = jnp.cos(turn)
    sin_t = jnp.sin(turn)
    flow_t = cos_t * blended[2] + sin_t * blended[3]
    flow_p = cos_t * blended[3] - sin_t * blended[2]
    field_t = cos_t * blended[5] + sin_t * blended[6]
    field_p = cos_t * blended[6] - sin_t * blended[5]
    return jnp.stack(
        [blended[0], blended[1], flow_t, flow_p, blended[4], field_t, field_p, blended[7]]
    )


def advance(padded, radius, sin_theta, d_theta, d_phi, dt_step, diffusivity):
    levels = padded.shape[1] - 2
    tile_rows = padded.shape[2] - 2
    tile_cols = padded.shape[3] - 2
    radial_h = 1.0 / DR_STEP
    colat_h = 1.0 / (radius[:, None, None] * d_theta)
    lon_h = 1.0 / (radius[:, None, None] * sin_theta[None, :, None] * d_phi)

    def shifted(field, step_r, step_t, step_p):
        return field[
            ...,
            1 + step_r : 1 + step_r + levels,
            1 + step_t : 1 + step_t + tile_rows,
            1 + step_p : 1 + step_p + tile_cols,
        ]

    def radial_diff(field):
        return (shifted(field, 1, 0, 0) - shifted(field, -1, 0, 0)) * (0.5 * radial_h)

    def colat_diff(field):
        return (shifted(field, 0, 1, 0) - shifted(field, 0, -1, 0)) * (0.5 * colat_h)

    def lon_diff(field):
        return (shifted(field, 0, 0, 1) - shifted(field, 0, 0, -1)) * (0.5 * lon_h)

    def laplace(field):
        centre = 2.0 * shifted(field, 0, 0, 0)
        return (
            (shifted(field, 1, 0, 0) + shifted(field, -1, 0, 0) - centre) * (radial_h * radial_h)
            + (shifted(field, 0, 1, 0) + shifted(field, 0, -1, 0) - centre) * (colat_h * colat_h)
            + (shifted(field, 0, 0, 1) + shifted(field, 0, 0, -1) - centre) * (lon_h * lon_h)
        )

    def cross_of(left_vec, right_vec):
        return jnp.stack(
            [
                left_vec[1] * right_vec[2] - left_vec[2] * right_vec[1],
                left_vec[2] * right_vec[0] - left_vec[0] * right_vec[2],
                left_vec[0] * right_vec[1] - left_vec[1] * right_vec[0],
            ]
        )

    def curl_of(field):
        return jnp.stack(
            [
                colat_diff(field[2]) - lon_diff(field[1]),
                lon_diff(field[0]) - radial_diff(field[2]),
                radial_diff(field[1]) - colat_diff(field[0]),
            ]
        )

    density_pad = padded[0]
    flow_pad = padded[1:4]
    magnet_pad = padded[4:7]
    press_pad = padded[7]
    density_c = shifted(density_pad, 0, 0, 0)
    flow_c = shifted(flow_pad, 0, 0, 0)
    magnet_c = shifted(magnet_pad, 0, 0, 0)
    press_c = shifted(press_pad, 0, 0, 0)
    momentum = density_pad[None] * flow_pad
    emf_pad = cross_of(flow_pad, magnet_pad)
    lorentz = cross_of(curl_of(magnet_pad), magnet_c)

    def carried(field):
        return (
            flow_c[0] * radial_diff(field)
            + flow_c[1] * colat_diff(field)
            + flow_c[2] * lon_diff(field)
        )

    div_mom = radial_diff(momentum[0]) + colat_diff(momentum[1]) + lon_diff(momentum[2])
    div_flow = radial_diff(flow_pad[0]) + colat_diff(flow_pad[1]) + lon_diff(flow_pad[2])
    press_grad = [radial_diff(press_pad), colat_diff(press_pad), lon_diff(press_pad)]
    new_density = density_c - dt_step * div_mom
    new_flow = jnp.stack(
        [
            flow_c[comp]
            + dt_step
            * (
                -carried(flow_pad[comp])
                + (lorentz[comp] - press_grad[comp]) / density_c
                + diffusivity * laplace(flow_pad[comp])
            )
            for comp in range(3)
        ]
    )
    new_magnet = magnet_c + dt_step * (curl_of(emf_pad) + diffusivity * laplace(magnet_pad))
    new_press = press_c + dt_step * (
        -carried(press_pad) - GAMMA * press_c * div_flow + diffusivity * laplace(press_pad)
    )
    return (new_density, new_flow, new_magnet, new_press)


def place_rows(target, wanted, values):
    hits = (target[:, None] == wanted[None, :]).astype(jnp.float32)
    return jnp.dot(
        hits.T, values, preferred_element_type=jnp.float32, precision=lax.Precision.HIGHEST
    )


def body(
    density, velocity, magnetic, pressure, send_row, send_col, send_weight, send_turn, send_dest
):
    fields = jnp.concatenate([density, velocity[0], magnetic[0], pressure], axis=0)
    levels = fields.shape[1]
    tile_rows = fields.shape[2]
    tile_cols = fields.shape[3]
    channels = 8 * levels
    theta_count = lax.axis_size("theta")
    phi_count = lax.axis_size(PHI)
    total_theta = tile_rows * theta_count
    total_phi = tile_cols * phi_count
    d_theta, d_phi, dt_step, diffusivity = grid_constants(total_theta, total_phi)
    patch_index = lax.axis_index("patch")
    theta_index = lax.axis_index("theta")
    phi_index = lax.axis_index(PHI)
    flattened = fields.reshape(channels, tile_rows * tile_cols)
    base_cell = send_row.reshape(-1) * tile_cols + send_col.reshape(-1)

    def corner(offset):
        return jnp.take(flattened, base_cell + offset, axis=1).reshape(8, levels, -1)

    weights = send_weight.reshape(2, -1)
    blended = bilinear(
        corner(0), corner(1), corner(tile_cols), corner(tile_cols + 1), weights[0], weights[1]
    )
    donor_rows = turn_frame(blended, send_turn.reshape(-1)).reshape(channels, -1).T
    target = send_dest.reshape(-1)
    lon_values = whole_of(donor_rows, PHI, 0)
    lon_targets = gathered_copies(target, PHI, 0)
    own_lon = phi_index * tile_cols + jnp.arange(tile_cols, dtype=jnp.int32)
    lon_part = jnp.concatenate(
        [
            place_rows(lon_targets, own_lon, lon_values),
            place_rows(lon_targets, own_lon + total_phi, lon_values),
        ],
        axis=1,
    )
    lat_ids = jnp.arange(total_theta, dtype=jnp.int32) + 2 * total_phi
    lat_full = jnp.concatenate(
        [
            place_rows(target, lat_ids, donor_rows),
            place_rows(target, lat_ids + total_theta, donor_rows),
        ],
        axis=1,
    )
    lat_part = sum_at_owner(lat_full, "theta", 0)
    slot_mask = (jnp.arange(2, dtype=jnp.int32) == 1 - patch_index)[:, None, None]
    lon_total = by_axis(jnp.where(slot_mask, lon_part[None], 0.0), ("patch", "theta"))
    lat_total = over_copies(jnp.where(slot_mask, lat_part[None], 0.0), PATCH_PHI)
    lon_border = lax.dynamic_index_in_dim(lon_total, patch_index, 0, keepdims=False)
    lat_border = lax.dynamic_index_in_dim(lat_total, patch_index, 0, keepdims=False)
    upper_side = lon_border[:, :channels].T.reshape(8, levels, tile_cols)
    lower_side = lon_border[:, channels:].T.reshape(8, levels, tile_cols)
    left_side = lat_border[:, :channels].T.reshape(8, levels, tile_rows)
    right_side = lat_border[:, channels:].T.reshape(8, levels, tile_rows)
    rims = extended(fields, (("theta", 2), (PHI, 3)), 1)
    padded = jnp.pad(rims, ((0, 0), (1, 1), (0, 0), (0, 0)), mode="edge")
    padded = padded.at[:, 1:-1, 0, 1:-1].set(
        jnp.where(theta_index == 0, upper_side, padded[:, 1:-1, 0, 1:-1])
    )
    padded = padded.at[:, 1:-1, -1, 1:-1].set(
        jnp.where(theta_index == theta_count - 1, lower_side, padded[:, 1:-1, -1, 1:-1])
    )
    padded = padded.at[:, 1:-1, 1:-1, 0].set(
        jnp.where(phi_index == 0, left_side, padded[:, 1:-1, 1:-1, 0])
    )
    padded = padded.at[:, 1:-1, 1:-1, -1].set(
        jnp.where(phi_index == phi_count - 1, right_side, padded[:, 1:-1, 1:-1, -1])
    )
    radius = R_BASE + (jnp.arange(levels, dtype=jnp.float32) + 0.5) * DR_STEP
    rows_global = theta_index * tile_rows + jnp.arange(tile_rows, dtype=jnp.int32)
    sin_theta = jnp.sin(0.25 * math.pi + (rows_global.astype(jnp.float32) + 0.5) * d_theta)
    new_density, new_flow, new_magnet, new_press = advance(
        padded, radius, sin_theta, d_theta, d_phi, dt_step, diffusivity
    )
    return (new_density[None], new_flow[None], new_magnet[None], new_press[None])


def solution(mesh):
    torus = Mesh(
        mesh.devices.reshape(mesh.shape["patch"], mesh.shape["theta"], 4, 4),
        ("patch", "theta", "phi_0", "phi_1"),
    )
    return jax.shard_map(
        body,
        mesh=torus,
        in_specs=(
            P("patch", None, "theta", PHI),
            P("patch", None, None, "theta", PHI),
            P("patch", None, None, "theta", PHI),
            P("patch", None, "theta", PHI),
            P("patch", "theta", PHI, None),
            P("patch", "theta", PHI, None),
            P("patch", "theta", PHI, None, None),
            P("patch", "theta", PHI, None),
            P("patch", "theta", PHI, None),
        ),
        out_specs=(
            P("patch", None, "theta", PHI),
            P("patch", None, None, "theta", PHI),
            P("patch", None, None, "theta", PHI),
            P("patch", None, "theta", PHI),
        ),
        check_vma=False,
    )
```

profile of v0, /device:TPU:32, one launch (start us, length us, event | category | flops | bytes accessed | tf_op | source)
XLA Modules:
  0.0 504.6 jit_solution(13883156774474768075)
XLA Ops:
  7.2 1.3 broadcast_in_dim.94
  8.4 7.0 %all-to-all-start = ((s32[16,1,96]{2,1,0:T(1,128)}), s32[16,1,96]{2,1,0:T(1,128)S(1)}, u32[]{:S(2)}, u32[]{:S(2)}) async-start(s32[16,1,96]{2,1,0:T(1,128)} %broadcast_in_dim.94), calls=%async_computation | async-start | bytes 16384 | tf_op jit(solution)/shard_map/all_to_all | solution.py:35
  15.5 0.7 compare_and_fusion.3
  16.2 0.8 broadcast_subtract_fusion.1
  16.9 0.8 slice_bitcast_fusion.19
  17.7 0.9 copy.131
  18.7 1.0 copy.132
  19.7 1.4 copy_bitcast_fusion.1
  21.8 1.3 copy.191
  23.2 1.5 copy.138
  24.7 0.6 gather_fusion.2
  25.5 0.6 gather_fusion.3
  26.4 0.6 gather_fusion.1
  27.2 0.6 gather_fusion
  28.9 1.0 copy.147
  29.9 28.7 %all-to-all-start.1 = ((f32[32,16,256]{2,1,0:T(8,128)}), f32[32,16,256]{2,1,0:T(8,128)}, u32[]{:S(2)}, u32[]{:S(2)}) async-start(f32[32,16,256]{2,1,0:T(8,128)} %bitcast.23), calls=%async_computation.1 | async-start | bytes 1048576 | tf_op jit(solution)/shard_map/all_to_all | solution.py:49
  58.6 0.7 fusion.66
  59.3 3.4 collective-permute-start.1
  62.6 1.4 fusion.65
  64.0 2.1 copy.133
  66.1 4.4 collective-permute-start
  70.5 0.9 copy.135
  71.3 1.3 collective-permute-start.3
  72.6 2.5 collective-permute-start.2
  75.2 13.1 %all_gather.6 = f32[384,128]{1,0:T(8,128)S(1)} all-gather(f32[96,128]{1,0:T(8,128)S(1)} %copy.146), channel_id=1, replica_groups=mesh['patch'=2,'theta'=32,'phi_0'=4,'phi_1'=4] {'phi_1'}, dimensions={0}, use_global_device_ids=true | all-gather | bytes 245760 | tf_op jit(solution)/shard_map/all_gather | solution.py:23
  89.1 15.3 %all_gather.7 = f32[1536,128]{1,0:T(8,128)S(1)} all-gather(f32[384,128]{1,0:T(8,128)S(1)} %all_gather.6), channel_id=1, replica_groups=mesh['patch'=2,'theta'=32,'phi_0'=4,'phi_1'=4] {'phi_0'}, dimensions={0}, use_global_device_ids=true | all-gather | bytes 983040 | tf_op jit(solution)/shard_map/all_gather | solution.py:23
  104.9 0.6 reduce.11
  105.6 1.0 fusion.2
  106.7 1.0 fusion
  107.7 0.8 broadcast_select_fusion
  108.6 2.7 copy.134
  111.3 1.4 pad.23
  112.7 1.9 copy.136
  114.6 1.3 pad.24
  116.1 0.9 copy-done.1
  117.0 1.0 pad_maximum_fusion.1
  118.0 0.9 fusion.64
  118.9 48.8 %all-reduce.5.cloned.1.call-done = f32[2,128,256]{1,2,0:T(8,128)} async-done(((f32[2,128,256]{1,2,0:T(8,128)}), f32[2,128,256]{1,2,0:T(8,128)}) %all-reduce.5.cloned.1.call-update) | async-done | bytes 262160 | tf_op jit(solution)/shard_map/psum | solution.py:55
  167.8 1.1 reduce_sum.18
  169.0 1.1 broadcast_in_dim.100
  170.1 7.4 %all-to-all-start.2 = ((f32[32,2,16,256]{3,2,1,0:T(8,128)}), f32[32,2,16,256]{3,2,1,0:T(8,128)}, u32[]{:S(2)}, u32[]{:S(2)}) async-start(f32[32,2,16,256]{3,2,1,0:T(8,128)} %broadcast_in_dim.100), calls=%async_computation.2 | async-start | bytes 2097152 | tf_op jit(solution)/shard_map/all_to_all | solution.py:35
  177.5 5.2 %pad_maximum_fusion = f32[8,18,18,130]{3,1,0,2:T(8,128)S(1)} fusion(f32[8,1,18,130]{3,1,0,2:T(1,128)} %get-tuple-element.94, f32[8,16,18,1]{3,1,0,2:T(8,128)} %copy-done.1, f32[8,16,1,128]{3,1,0,2:T(8,128)} %copy-done.7, f32[1,16,16,128]{3,1,0,2:T(8,128)} %copy-done.5, f32[3,16,16,128]{3,1,0,2:T(8,128)} %copy-done.2, f32[3,16,16,128]{3,1,0,2:T(8,128)} %copy-done.3, ...), kind=kLoop, calls=%fused_computation.4 | loop fusion | flops 3032640 | bytes 2695680 | tf_op jit(solution)/shard_map/jit(_pad)/concatenate | solution.py:270
  182.7 253.5 %all-reduce.7.cloned.1.call-done = f32[2,128,256]{1,2,0:T(8,128)} async-done(((f32[2,128,256]{1,2,0:T(8,128)}), f32[2,128,256]{1,2,0:T(8,128)}) %all-reduce.7.cloned.1.call-update) | async-done | bytes 262160 | tf_op jit(solution)/shard_map/psum | solution.py:55
  436.2 0.9 dynamic-slice_bitcast_fusion
  437.2 0.6 fusion.67
  437.8 1.5 broadcast_select_fusion.1
  439.3 3.7 scatter.14
  443.0 0.7 slice_select_fusion.2
  443.7 3.7 scatter.15
  447.4 1.9 reduce_sum.19
  449.3 0.7 dynamic-slice_bitcast_fusion.1
  450.6 2.5 reshape.508
  453.2 2.4 slice_select_fusion.1
  455.6 6.1 %scatter.16 = f32[8,18,18,130]{3,1,0,2:T(8,128)S(1)} dynamic-update-slice(f32[8,18,18,130]{3,1,0,2:T(8,128)S(1)} %scatter.15, f32[8,16,16,1]{3,1,0,2:T(8,128)} %slice_select_fusion.1, s32[]{:T(128)} %constant.204.clone.1, s32[]{:T(128)} %constant.205.clone.1, s32[]{:T(128)} %constant.205.clone.1, s32[]{:T(128)} %constant.204.clone.1) | dynamic-update-slice | bytes 16388 | tf_op jit(solution)/shard_map/scatter | solution.py:277
  461.7 2.6 reshape.509
  464.3 1.3 slice_select_fusion
  465.6 23.4 %scatter.19 = f32[8,18,18,130]{3,1,0,2:T(8,128)S(1)} dynamic-update-slice(f32[8,18,18,130]{3,1,0,2:T(8,128)S(1)} %scatter.16, f32[8,16,16,1]{3,1,0,2:T(8,128)} %slice_select_fusion, s32[]{:T(128)} %constant.204.clone.1, s32[]{:T(128)} %constant.205.clone.1, s32[]{:T(128)} %constant.205.clone.1, s32[]{:T(128)} %constant.213.clone.1) | dynamic-update-slice | bytes 16388 | tf_op jit(solution)/shard_map/scatter | solution.py:280
  490.7 0.7 copy.170
  491.8 0.7 fusion.11
  492.5 0.9 copy.169
  493.6 0.9 add_bitcast_fusion.3
  494.4 0.7 add_bitcast_fusion.2
  495.8 0.9 copy.168
  497.1 0.7 copy.167
  (82 shorter events, 7.7 us)
Async XLA Ops:
  8.4 21.5 %all-to-all-start = ((s32[16,1,96]{2,1,0:T(1,128)}), s32[16,1,96]{2,1,0:T(1,128)S(1)}, u32[]{:S(2)}, u32[]{:S(2)}) async-start(s32[16,1,96]{2,1,0:T(1,128)} %broadcast_in_dim.94), calls=%async_computation | async-start | bytes 16384 | tf_op jit(solution)/shard_map/all_to_all | solution.py:35
  18.6 97.4 %copy-start.4 = (f32[1,16,16,128]{3,1,0,2:T(8,128)}, f32[1,16,16,128]{3,1,0,2:T(8,128)S(1)}, u32[]{:S(2)}) copy-start(f32[1,16,16,128]{3,1,0,2:T(8,128)S(1)} %copy.131) | copy-start | bytes 393220
  19.7 96.4 %copy-start.5 = (f32[1,16,16,128]{3,1,0,2:T(8,128)}, f32[1,16,16,128]{3,1,0,2:T(8,128)S(1)}, u32[]{:S(2)}) copy-start(f32[1,16,16,128]{3,1,0,2:T(8,128)S(1)} %copy.132) | copy-start | bytes 393220
  21.1 95.0 %copy-start.2 = (f32[3,16,16,128]{3,1,0,2:T(8,128)}, f32[3,16,16,128]{3,1,0,2:T(8,128)S(1)}, u32[]{:S(2)}) copy-start(f32[3,16,16,128]{3,1,0,2:T(8,128)S(1)} %get-tuple-element.121) | copy-start | bytes 1179652
  21.1 95.0 %copy-start.3 = (f32[3,16,16,128]{3,1,0,2:T(8,128)}, f32[3,16,16,128]{3,1,0,2:T(8,128)S(1)}, u32[]{:S(2)}) copy-start(f32[3,16,16,128]{3,1,0,2:T(8,128)S(1)} %get-tuple-element.122) | copy-start | bytes 1179652
  21.8 6.2 %copy-start.11 = (f32[1,1,1,96]{3,2,1,0:T(1,128)S(1)}, f32[1,1,1,96]{3,2,1,0:T(1,128)}, u32[]{:S(2)}) copy-start(f32[1,1,1,96]{3,2,1,0:T(1,128)} %param.26) | copy-start | bytes 1156
  21.8 6.3 %copy-start.10 = (s32[1,1,1,96]{3,2,1,0:T(1,128)S(1)}, s32[1,1,1,96]{3,2,1,0:T(1,128)}, u32[]{:S(2)}) copy-start(s32[1,1,1,96]{3,2,1,0:T(1,128)} %param.27) | copy-start | bytes 1156
  29.9 137.9 %all-to-all-start.1 = ((f32[32,16,256]{2,1,0:T(8,128)}), f32[32,16,256]{2,1,0:T(8,128)}, u32[]{:S(2)}, u32[]{:S(2)}) async-start(f32[32,16,256]{2,1,0:T(8,128)} %bitcast.23), calls=%async_computation.1 | async-start | bytes 1048576 | tf_op jit(solution)/shard_map/all_to_all | solution.py:49
  58.6 109.2 %all-reduce.5.cloned.1.call-start = ((), (), s32[]{:S(2)}) async-start(), calls=%async_computation.3 | async-start | bytes 524288 | tf_op jit(solution)/shard_map/psum | solution.py:55
  59.3 56.7 %collective-permute-start.1 = (f32[8,16,1,128]{3,1,0,2:T(8,128)}, f32[8,16,1,128]{3,1,0,2:T(8,128)S(1)}, u32[]{:S(2)}, u32[]{:S(2)}) collective-permute-start(f32[8,16,1,128]{3,1,0,2:T(8,128)} %get-tuple-element.100), channel_id=1, source_target_pairs={{0,16},{16,32},{32,48},{48,64},{64,80},{80,96},{96,112},{112,128},... | collective-permute-start | bytes 196616 | tf_op jit(solution)/shard_map/ppermute | solution.py:71
  66.1 42.5 %collective-permute-start = (f32[8,16,16,1]{2,1,3,0:T(8,128)S(1)}, f32[8,16,16,1]{2,1,3,0:T(8,128)}, u32[]{:S(2)}, u32[]{:S(2)}) collective-permute-start(f32[8,16,16,1]{2,1,3,0:T(8,128)S(1)} %copy.133), channel_id=1, source_target_pairs={{0,1},{1,2},{2,3},{3,4},{4,5},{5,6},{6,7},{7,8},{8,9},{9,10},{10,1... | collective-permute-start | bytes 24584 | tf_op jit(solution)/shard_map/ppermute | solution.py:71
  71.3 41.4 %collective-permute-start.3 = (f32[8,16,16,1]{2,1,3,0:T(8,128)S(1)}, f32[8,16,16,1]{2,1,3,0:T(8,128)S(1)}, u32[]{:S(2)}, u32[]{:S(2)}) collective-permute-start(f32[8,16,16,1]{2,1,3,0:T(8,128)S(1)} %copy.135), channel_id=1, source_target_pairs={{1,0},{2,1},{3,2},{4,3},{5,4},{6,5},{7,6},{8,7},{9,8},{10,9},{11,1... | collective-permute-start | bytes 24584 | tf_op jit(solution)/shard_map/ppermute | solution.py:72
  72.6 43.4 %collective-permute-start.2 = (f32[8,16,1,128]{3,1,0,2:T(8,128)}, f32[8,16,1,128]{3,1,0,2:T(8,128)S(1)}, u32[]{:S(2)}, u32[]{:S(2)}) collective-permute-start(f32[8,16,1,128]{3,1,0,2:T(8,128)} %get-tuple-element.101), channel_id=1, source_target_pairs={{16,0},{32,16},{48,32},{64,48},{80,64},{96,80},{112,96},{128,112},... | collective-permute-start | bytes 196616 | tf_op jit(solution)/shard_map/ppermute | solution.py:72
  108.5 327.7 %all-reduce.7.cloned.1.call-start = ((), (), s32[]{:S(2)}) async-start(), calls=%async_computation.4 | async-start | bytes 524288 | tf_op jit(solution)/shard_map/psum | solution.py:55
  112.7 5.3 %copy-start = (f32[8,16,18,1]{3,1,0,2:T(8,128)}, f32[8,16,18,1]{3,1,0,2:T(8,128)S(1)}, u32[]{:S(2)}) copy-start(f32[8,16,18,1]{3,1,0,2:T(8,128)S(1)} %pad.23) | copy-start | bytes 27652
  116.0 1.0 copy-start.1
  116.0 52.9 %copy-start.6 = (f32[8,16,1,128]{3,1,0,2:T(8,128)}, f32[8,16,1,128]{3,1,0,2:T(8,128)S(1)}, u32[]{:S(2)}) copy-start(f32[8,16,1,128]{3,1,0,2:T(8,128)S(1)} %collective-permute-done.1) | copy-start | bytes 196612
  117.0 51.9 %copy-start.7 = (f32[8,16,1,128]{3,1,0,2:T(8,128)}, f32[8,16,1,128]{3,1,0,2:T(8,128)S(1)}, u32[]{:S(2)}) copy-start(f32[8,16,1,128]{3,1,0,2:T(8,128)S(1)} %collective-permute-done.2) | copy-start | bytes 196612
  170.1 277.3 %all-to-all-start.2 = ((f32[32,2,16,256]{3,2,1,0:T(8,128)}), f32[32,2,16,256]{3,2,1,0:T(8,128)}, u32[]{:S(2)}, u32[]{:S(2)}) async-start(f32[32,2,16,256]{3,2,1,0:T(8,128)} %broadcast_in_dim.100), calls=%async_computation.2 | async-start | bytes 2097152 | tf_op jit(solution)/shard_map/all_to_all | solution.py:35
  489.4 0.6 copy-start.8
  489.4 0.6 copy-start.9
Sparse Core Ops, SparseCore 0:
  108.6 59.0 all-reduce.4
  170.1 266.1 all-reduce.6
where the time goes:
time: 506 us; the launch traced here: 505 us
  waiting for transfers between devices  302 us (60%)
  local copies, waits for them, and re-layouts  77.7 us (15%)
  starting transfers between devices  54.7 us (11%)
  blocking collectives  28.4 us (6%)
  other arithmetic  23.9 us (5%)
  between operations  14.7 us (3%)
    psum x2, waiting for transfers between devices, by_axis(): value = lax.psum(value, axis)  302 us
    all_to_all x1, starting transfers between devices, sum_at_owner(): lax.all_to_all(pieces, axis, split_axis=0, concat_axis=0, tiled=True)  28.7 us
    all_gather x2, blocking collectives, whole_of(): out = lax.all_gather(out, axes[number], axis=dim, tiled=True)  28.4 us
    scatter x1, local copies, waits for them, and re-layouts, body(): padded.at[:, 1:-1, 1:-1, -1]  23.4 us
    all_to_all x2, starting transfers between devices, sent_to_all(): return lax.all_to_all(copies, axis, split_axis=0, concat_axis=0, tiled=True)  14.4 us
  transfers between devices with their start and end apart: 9, of which 2 were waited for; matrix products, arithmetic and copies ran while one was open for 10% of the time, Pallas kernels for 0%

commit v1 on v0

v1 whole, which is shorter than its diff:
```python
import functools
import math

import jax
import jax.numpy as jnp
from jax import lax
from jax.experimental import pallas as pl
from jax.experimental.pallas import tpu as pltpu
from jax.sharding import PartitionSpec as P

MESH = pl.DeviceIdType.MESH
F32 = jnp.float32
BF16 = jnp.bfloat16

GAMMA = 5.0 / 3.0
R_BASE = 0.6
DR_STEP = 0.65 / 64.0
COURANT = 0.4
DIFFUSE = 0.4

NR, CT, CP = 16, 16, 128
NZ, NF = 32, 16
NPH, NTH = CP * NF, CT * NZ
SEND = 96
CH = 8 * NR
HUBS = (0, NZ - 1, 8, 24)
SOURCES = 2 * NF + 2 * (NZ - 2)
SLOT_ROWS = 96 * 8


def grid_constants(total_theta, total_phi):
    d_theta = 0.5 * math.pi / total_theta
    d_phi = 1.5 * math.pi / total_phi
    r_low = R_BASE + 0.5 * DR_STEP
    inv_r = 1.0 / DR_STEP
    inv_t = 1.0 / (r_low * d_theta)
    inv_p = 1.0 / (r_low * math.sin(0.25 * math.pi) * d_phi)
    dt_step = COURANT / (inv_r + inv_t + inv_p)
    diffusivity = DIFFUSE / (dt_step * (inv_r * inv_r + inv_t * inv_t + inv_p * inv_p))
    return (d_theta, d_phi, dt_step, diffusivity)


def components(dens, vel, mag, pres):
    return [dens, vel.at[0], vel.at[1], vel.at[2], mag.at[0], mag.at[1], mag.at[2], pres]


def iota(shape, dim):
    return lax.broadcasted_iota(jnp.int32, shape, dim)


def pack_kernel(
    dens, vel, mag, pres, row_in, col_in, weight_in, turn_in, dest_in,
    first_row, last_row, left_col, right_col, donors, ints, floats,
):
    z = lax.axis_index("theta")
    f = lax.axis_index("phi")
    comps = components(dens, vel, mag, pres)
    for c in range(8):
        first_row[c * NR : (c + 1) * NR, :] = comps[c][:, 0, :]
        last_row[c * NR : (c + 1) * NR, :] = comps[c][:, CT - 1, :]
    lane = iota((CT, CP), 1)
    low = jnp.zeros((CT, CP), F32)
    high = jnp.zeros((CT, CP), F32)
    for c in range(8):
        for k in range(NR):
            ck = c * NR + k
            block = comps[c][k]
            low = jnp.where(lane == ck, pltpu.roll(block, ck, 1) if ck else block, low)
            shift = (ck + 1) % CP
            high = jnp.where(lane == ck, pltpu.roll(block, shift, 1) if shift else block, high)
    left_col[...] = low
    right_col[...] = high

    @pl.when((z == 0) | (z == NZ - 1) | (f == 0) | (f == NF - 1))
    def _():
        ints[...] = jnp.zeros_like(ints)
        floats[...] = jnp.zeros_like(floats)
        ints[0:1, 0:SEND] = row_in[...]
        ints[1:2, 0:SEND] = col_in[...]
        ints[2:3, 0:SEND] = jnp.where(dest_in[...] < 2 * (NPH + NTH), dest_in[...] + 1, 0)
        floats[0:2, 0:SEND] = weight_in[...]
        floats[2:3, 0:SEND] = turn_in[...]
        row, col, dest = ints[0:1, :], ints[1:2, :], ints[2:3, :]
        weight_row, weight_col, turn = floats[0:1, :], floats[1:2, :], floats[2:3, :]
        cell = iota((CP, CP), 0)
        col_mix = jnp.where(cell == col, 1.0 - weight_col, 0.0) + jnp.where(
            cell == col + 1, weight_col, 0.0
        )
        level = iota((CT, CP), 0)
        row_mix = jnp.where(level == row, 1.0 - weight_row, 0.0) + jnp.where(
            level == row + 1, weight_row, 0.0
        )
        value = jnp.zeros((CH, CP), F32)
        for i in range(CT):
            line = jnp.concatenate([comps[c][:, i, :] for c in range(8)], axis=0)
            mixed = jnp.dot(
                line, col_mix, preferred_element_type=F32, precision=lax.Precision.HIGHEST
            )
            value = value + row_mix[i : i + 1, :] * mixed
        cos_t, sin_t = jnp.cos(turn), jnp.sin(turn)
        part = [value[c * NR : (c + 1) * NR, :] for c in range(8)]
        turned = jnp.concatenate(
            [
                part[0],
                part[1],
                cos_t * part[2] + sin_t * part[3],
                cos_t * part[3] - sin_t * part[2],
                part[4],
                cos_t * part[5] + sin_t * part[6],
                cos_t * part[6] - sin_t * part[5],
                part[7],
            ],
            axis=0,
        )
        slots = turned.T
        for r in range(6):
            donors[pl.ds(r, 16, stride=8), :] = slots[16 * r : 16 * r + 16, :]
        where_z = jnp.where(z == 0, f, jnp.where(z == NZ - 1, NF + f, 0))
        where_f = jnp.where(f == 0, 2 * NF + z - 1, 2 * NF + NZ - 2 + z - 1)
        source = jnp.where((z == 0) | (z == NZ - 1), where_z, where_f)
        base = 8 * lax.rem(source, 16)
        slot = iota((16, CP), 1)
        group = iota((16, CP), 0)
        named = jnp.where(lax.rem(slot, 16) == group, dest.astype(F32), 0.0)
        slot_down = iota((CP, CP), 0)
        placed = jnp.where(iota((CP, CP), 1) == base + slot_down // 16, 1.0, 0.0)
        donors[pl.ds(6, 16, stride=8), :] = jnp.dot(
            named, placed, preferred_element_type=F32, precision=lax.Precision.HIGHEST
        )
        donors[pl.ds(7, 16, stride=8), :] = jnp.zeros((16, CP), F32)


def route_kernel(
    first_row, last_row, left_col, right_col, donors,
    out_top, out_bottom, out_left, out_right,
    top, bottom, left, right, slots, pieces, dense, inbox, total,
    halo_send, halo_recv, donor_send, donor_recv, dense_send, dense_recv, column_send,
):
    p = lax.axis_index("patch")
    z = lax.axis_index("theta")
    f = lax.axis_index("phi")
    on_row = (z == 0) | (z == NZ - 1)
    on_column = (f == 0) | (f == NF - 1)
    is_source = on_row | on_column
    column_hub = (z == HUBS[2]) | (z == HUBS[3])
    is_hub = on_row | column_hub
    half = z // 16
    hub_low = 16 * (z // 16)

    barrier = pltpu.get_barrier_semaphore()

    def greet(device):
        pl.semaphore_signal(barrier, inc=1, device_id=device, device_id_type=MESH)

    for has, device in (
        (z > 0, (p, z - 1, f)),
        (z < NZ - 1, (p, z + 1, f)),
        (f > 0, (p, z, f - 1)),
        (f < NF - 1, (p, z, f + 1)),
    ):
        pl.when(has)(functools.partial(greet, device))

    @pl.when(is_hub)
    def _():
        @pl.loop(0, NF)
        def _(j):
            greet((1 - p, 0, j))
            greet((1 - p, NZ - 1, j))

        @pl.loop(1, NZ - 1)
        def _(j):
            greet((1 - p, j, 0))
            greet((1 - p, j, NF - 1))

        @pl.loop(1, NF)
        def _(off):
            greet((p, z, lax.rem(f + off, NF)))

    @pl.when(on_column)
    def _():
        greet((p, HUBS[2] + 16 * half, z - 16 * half))

    @pl.when(is_hub)
    def _():
        slots[8 * SOURCES : SLOT_ROWS, :] = jnp.zeros((SLOT_ROWS - 8 * SOURCES, CP), F32)

    peers = (
        jnp.where(z > 0, 1, 0)
        + jnp.where(z < NZ - 1, 1, 0)
        + jnp.where(f > 0, 1, 0)
        + jnp.where(f < NF - 1, 1, 0)
        + jnp.where(is_hub, NF - 1, 0)
        + jnp.where(column_hub, 2, 0)
        + jnp.where(is_source, 4 * NF, 0)
    )
    pl.semaphore_wait(barrier, peers)

    def halo(which):
        src, dst, device = (
            (last_row, top, (p, z + 1, f)),
            (first_row, bottom, (p, z - 1, f)),
            (right_col, left, (p, z, f + 1)),
            (left_col, right, (p, z, f - 1)),
        )[which]
        return pltpu.make_async_remote_copy(
            src_ref=src,
            dst_ref=dst,
            send_sem=halo_send.at[which],
            recv_sem=halo_recv.at[which],
            device_id=device,
            device_id_type=MESH,
        )

    sends_to = (z < NZ - 1, z > 0, f < NF - 1, f > 0)
    hears_from = (z > 0, z < NZ - 1, f > 0, f < NF - 1)

    source = jnp.where(
        z == 0,
        f,
        jnp.where(z == NZ - 1, NF + f, jnp.where(f == 0, 2 * NF + z - 1, 2 * NF + NZ - 3 + z)),
    )

    def donor_copy(hub, plane, j):
        return pltpu.make_async_remote_copy(
            src_ref=donors.at[pl.ds(pl.multiple_of(8 * j, 8), 8)],
            dst_ref=slots.at[pl.ds(pl.multiple_of(8 * source, 8), 8)],
            send_sem=donor_send.at[hub],
            recv_sem=donor_recv,
            device_id=(1 - p, plane, j),
            device_id_type=MESH,
        )

    @pl.when(is_source)
    def _():
        @pl.loop(0, NF)
        def _(off):
            j = lax.rem(f + off, NF)
            for hub, plane in enumerate(HUBS):
                donor_copy(hub, plane, j).start()

    for which in range(4):

        @pl.when(sends_to[which])
        def _():
            halo(which).start()

    def whole_wait(ref, sem):
        return pltpu.make_async_copy(ref, ref, sem).wait()

    def split_slots():
        value = slots[...]
        high = value.astype(BF16)
        rest = value - high.astype(F32)
        mid = rest.astype(BF16)
        pieces[:, 0:CP] = high
        pieces[:, CP : 2 * CP] = mid
        pieces[:, 2 * CP :] = (rest - mid.astype(F32)).astype(BF16)
        ids = slots[pl.ds(6, 96, stride=8), :]
        return jnp.concatenate(
            [jnp.sum(ids[16 * g : 16 * g + 16, :], axis=0, keepdims=True) for g in range(6)],
            axis=1,
        )

    def place(ids, wanted):
        hits = jnp.where(ids == wanted.astype(F32), 1.0, 0.0).astype(BF16)
        out = jnp.dot(hits, pieces[...], preferred_element_type=F32)
        return out[:, 0:CP] + out[:, CP : 2 * CP] + out[:, 2 * CP :]

    point = iota((CP, 1), 0)

    def block_copy(rows, j):
        return pltpu.make_async_remote_copy(
            src_ref=dense.at[pl.ds(pl.multiple_of(rows * j, rows), rows)],
            dst_ref=inbox.at[pl.ds(pl.multiple_of(rows * f, rows), rows)],
            send_sem=dense_send,
            recv_sem=dense_recv,
            device_id=(p, z, j),
            device_id_type=MESH,
        )

    def gather_blocks(rows):
        whole_wait(inbox.at[pl.ds(0, rows * (NF - 1))], dense_recv)
        own = dense[pl.ds(pl.multiple_of(rows * f, rows), rows), :]

        def step(off, acc):
            j = lax.rem(f + off, NF)
            return acc + inbox[pl.ds(pl.multiple_of(rows * j, rows), rows), :]

        return lax.fori_loop(1, NF, step, own)

    @pl.when(on_row)
    def _():
        whole_wait(slots.at[pl.ds(0, 8 * SOURCES)], donor_recv)
        ids = split_slots()
        first = 1 + jnp.where(z == 0, 0, NPH)

        @pl.loop(1, NF + 1)
        def _(off):
            j = lax.rem(f + off, NF)
            dense[pl.ds(pl.multiple_of(CP * j, CP), CP), :] = place(ids, first + CP * j + point)

            @pl.when(off > 1)
            def _():
                block_copy(CP, lax.rem(f + off - 1, NF)).start()

        border = gather_blocks(CP).T

        @pl.when(z == 0)
        def _():
            top[...] = border

        @pl.when(z == NZ - 1)
        def _():
            bottom[...] = border

        whole_wait(dense.at[pl.ds(0, CP * (NF - 1))], dense_send)

    @pl.when(column_hub)
    def _():
        whole_wait(slots.at[pl.ds(0, 8 * SOURCES)], donor_recv)
        ids = split_slots()
        side = lax.rem(point, 32) // 16
        first = 1 + 2 * NPH + NTH * side + lax.rem(point, 16) + CT * (hub_low + point // 32)

        @pl.loop(0, 4)
        def _(quad):
            dense[pl.ds(pl.multiple_of(CP * quad, CP), CP), :] = place(ids, first + CT * 4 * quad)

        @pl.loop(1, NF)
        def _(off):
            block_copy(32, lax.rem(f + off, NF)).start()

        total[...] = gather_blocks(32)

        def forward(side_of, dst):
            return pltpu.make_async_remote_copy(
                src_ref=total.at[pl.ds(16 * side_of, 16)],
                dst_ref=dst,
                send_sem=column_send.at[side_of],
                recv_sem=halo_recv.at[2 + side_of],
                device_id=(p, hub_low + f, (NF - 1) * side_of),
                device_id_type=MESH,
            )

        copies = [forward(0, left), forward(1, right)]
        for copy in copies:
            copy.start()
        whole_wait(dense.at[pl.ds(0, 32 * (NF - 1))], dense_send)
        for copy in copies:
            copy.wait_send()

    for which, ref in enumerate((top, bottom)):

        @pl.when(hears_from[which])
        def _():
            whole_wait(ref, halo_recv.at[which])

    for which, ref in ((2, left), (3, right)):
        whole_wait(ref, halo_recv.at[which])

    out_top[...] = top[...]
    out_bottom[...] = bottom[...]
    out_left[...] = left[...]
    out_right[...] = right[...]

    for which in range(4):

        @pl.when(sends_to[which])
        def _():
            halo(which).wait_send()

    @pl.when(is_source)
    def _():
        for hub in range(4):
            whole_wait(donors, donor_send.at[hub])


def step_kernel(
    constants, dens, vel, mag, pres, top, bottom, left, right,
    new_dens, new_vel, new_mag, new_pres,
):
    d_theta, d_phi, dt, nu = constants
    z = lax.axis_index("theta")
    comps = components(dens, vel, mag, pres)
    row = iota((CT, CP), 0)
    lane = iota((CT, CP), 1)
    angle = 0.25 * math.pi + ((z * CT + row).astype(F32) + 0.5) * d_theta
    inv_sin = 1.0 / jnp.sin(angle)
    inv_sin_sq = inv_sin * inv_sin
    left_all, right_all = left[...], right[...]
    gr = 1.0 / DR_STEP

    for k in range(NR):
        radius = R_BASE + (k + 0.5) * DR_STEP
        gt = 1.0 / (radius * d_theta)
        gp = 1.0 / (radius * d_phi)
        hr, ht, hp = 0.5 * gr, 0.5 * gt, (0.5 * gp) * inv_sin
        lr, lt, lp = nu * gr * gr, nu * gt * gt, (nu * gp * gp) * inv_sin_sq
        C, U, D, N, S, W, E = ([], [], [], [], [], [], [])
        for c in range(8):
            ck = c * NR + k
            here = comps[c][k]
            C.append(here)
            U.append(comps[c][min(k + 1, NR - 1)])
            D.append(comps[c][max(k - 1, 0)])
            N.append(jnp.where(row == 0, top[ck : ck + 1, :], pltpu.roll(here, 1, 0)))
            S.append(jnp.where(row == CT - 1, bottom[ck : ck + 1, :], pltpu.roll(here, CT - 1, 0)))
            shift_w, shift_e = (CP - ck) % CP, (CP - 1 - ck) % CP
            edge_w = pltpu.roll(left_all, shift_w, 1) if shift_w else left_all
            edge_e = pltpu.roll(right_all, shift_e, 1) if shift_e else right_all
            W.append(jnp.where(lane == 0, edge_w, pltpu.roll(here, 1, 1)))
            E.append(jnp.where(lane == CP - 1, edge_e, pltpu.roll(here, CP - 1, 1)))

        def dr(c):
            return (U[c] - D[c]) * hr

        def dt_(c):
            return (S[c] - N[c]) * ht

        def dp(c):
            return (E[c] - W[c]) * hp

        def laplace(c):
            twice = 2.0 * C[c]
            return (
                (U[c] + D[c] - twice) * lr
                + (S[c] + N[c] - twice) * lt
                + (E[c] + W[c] - twice) * lp
            )

        def emf(side, comp):
            a, b = (((2, 6), (3, 5)), ((3, 4), (1, 6)), ((1, 5), (2, 4)))[comp]
            return side[a[0]] * side[a[1]] - side[b[0]] * side[b[1]]

        rho, p = C[0], C[7]
        v = C[1:4]
        b = C[4:7]
        grad_v = [(dr(c), dt_(c), dp(c)) for c in (1, 2, 3)]
        grad_p = (dr(7), dt_(7), dp(7))
        div_mom = (
            (U[0] * U[1] - D[0] * D[1]) * hr
            + (S[0] * S[2] - N[0] * N[2]) * ht
            + (E[0] * E[3] - W[0] * W[3]) * hp
        )
        new_dens[k] = rho - dt * div_mom
        j_r = dt_(6) - dp(5)
        j_t = dp(4) - dr(6)
        j_p = dr(5) - dt_(4)
        force = (j_t * b[2] - j_p * b[1], j_p * b[0] - j_r * b[2], j_r * b[1] - j_t * b[0])
        inv_rho = 1.0 / rho

        def carried(grad):
            return v[0] * grad[0] + v[1] * grad[1] + v[2] * grad[2]

        for c in range(3):
            new_vel[c, k] = v[c] + dt * (
                (force[c] - grad_p[c]) * inv_rho - carried(grad_v[c]) + laplace(1 + c)
            )
        div_v = grad_v[0][0] + grad_v[1][1] + grad_v[2][2]
        new_pres[k] = p + dt * (laplace(7) - carried(grad_p) - GAMMA * p * div_v)
        dt_ep = (emf(S, 2) - emf(N, 2)) * ht
        dp_et = (emf(E, 1) - emf(W, 1)) * hp
        dp_er = (emf(E, 0) - emf(W, 0)) * hp
        dr_ep = (emf(U, 2) - emf(D, 2)) * hr
        dr_et = (emf(U, 1) - emf(D, 1)) * hr
        dt_er = (emf(S, 0) - emf(N, 0)) * ht
        new_mag[0, k] = b[0] + dt * (dt_ep - dp_et + laplace(4))
        new_mag[1, k] = b[1] + dt * (dp_er - dr_ep + laplace(5))
        new_mag[2, k] = b[2] + dt * (dr_et - dt_er + laplace(6))


VMEM = pl.BlockSpec(memory_space=pltpu.VMEM)


def shape(*dims):
    return jax.ShapeDtypeStruct(dims, F32)


def body(
    density, velocity, magnetic, pressure, send_row, send_col, send_weight, send_turn, send_dest
):
    fields = (density[0], velocity[0], magnetic[0], pressure[0])
    packed = pl.pallas_call(
        pack_kernel,
        out_shape=(shape(CH, CP), shape(CH, CP), shape(CT, CP), shape(CT, CP), shape(CP, CP)),
        in_specs=[VMEM] * 9,
        out_specs=(VMEM,) * 5,
        scratch_shapes=[pltpu.VMEM((8, CP), jnp.int32), pltpu.VMEM((8, CP), F32)],
        name="pack",
    )(
        *fields,
        send_row.reshape(1, SEND),
        send_col.reshape(1, SEND),
        send_weight.reshape(2, SEND),
        send_turn.reshape(1, SEND),
        send_dest.reshape(1, SEND),
    )
    halos = pl.pallas_call(
        route_kernel,
        out_shape=(shape(CH, CP), shape(CH, CP), shape(CT, CP), shape(CT, CP)),
        in_specs=[VMEM] * 5,
        out_specs=(VMEM,) * 4,
        scratch_shapes=[
            pltpu.VMEM((CH, CP), F32),
            pltpu.VMEM((CH, CP), F32),
            pltpu.VMEM((CT, CP), F32),
            pltpu.VMEM((CT, CP), F32),
            pltpu.VMEM((SLOT_ROWS, CP), F32),
            pltpu.VMEM((SLOT_ROWS, 3 * CP), BF16),
            pltpu.VMEM((NF * CP, CP), F32),
            pltpu.VMEM((NF * CP, CP), F32),
            pltpu.VMEM((32, CP), F32),
            pltpu.SemaphoreType.DMA((4,)),
            pltpu.SemaphoreType.DMA((4,)),
            pltpu.SemaphoreType.DMA((4,)),
            pltpu.SemaphoreType.DMA,
            pltpu.SemaphoreType.DMA,
            pltpu.SemaphoreType.DMA,
            pltpu.SemaphoreType.DMA((2,)),
        ],
        compiler_params=pltpu.CompilerParams(collective_id=0, has_side_effects=True),
        name="route",
    )(*packed)
    new_density, new_flow, new_magnet, new_press = pl.pallas_call(
        functools.partial(step_kernel, grid_constants(NTH, NPH)),
        out_shape=(shape(NR, CT, CP), shape(3, NR, CT, CP), shape(3, NR, CT, CP), shape(NR, CT, CP)),
        in_specs=[VMEM] * 8,
        out_specs=(VMEM,) * 4,
        name="step",
    )(*fields, *halos)
    return (new_density[None], new_flow[None], new_magnet[None], new_press[None])


def solution(mesh):
    return jax.shard_map(
        body,
        mesh=mesh,
        in_specs=(
            P("patch", None, "theta", "phi"),
            P("patch", None, None, "theta", "phi"),
            P("patch", None, None, "theta", "phi"),
            P("patch", None, "theta", "phi"),
            P("patch", "theta", "phi", None),
            P("patch", "theta", "phi", None),
            P("patch", "theta", "phi", None, None),
            P("patch", "theta", "phi", None),
            P("patch", "theta", "phi", None),
        ),
        out_specs=(
            P("patch", None, "theta", "phi"),
            P("patch", None, None, "theta", "phi"),
            P("patch", None, None, "theta", "phi"),
            P("patch", None, "theta", "phi"),
        ),
        check_vma=False,
    )
```

time: 506 us -> 111 us (0.22)
  the two profiles are of different devices: /device:TPU:32 before, /device:TPU:1 now
where the time goes in v1:
time: 111 us; the launch traced here: 110 us
  Pallas kernels  110 us (99%)
    pallas_call x1, Pallas kernels, body(): pl.pallas_call(route_kernel, out_shape=(shape(CH, CP), shape(CH, CP), sha...  102 us
    pallas_call x1, Pallas kernels, body(): pl.pallas_call(pack_kernel, out_shape=(shape(CH, CP), shape(CH, CP), shap...  3.85 us
    pallas_call x1, Pallas kernels, body(): pl.pallas_call(functools.partial(step_kernel, grid_constants(NTH, NPH)),...  3.72 us

profile of v1, /device:TPU:1, one launch (start us, length us, event | category | flops | bytes accessed | tf_op | source)
XLA Modules:
  0.0 110.2 jit_solution(194169613627715519)
XLA Ops:
  0.6 3.8 %pack.1 = (f32[128,128]{1,0:T(8,128)}, f32[128,128]{1,0:T(8,128)}, f32[16,128]{1,0:T(8,128)}, f32[16,128]{1,0:T(8,128)}, f32[128,128]{1,0:T(8,128)}) custom-call(f32[16,16,128]{2,1,0:T(8,128)} %bitcast.17, f32[3,16,16,128]{3,2,1,0:T(8,128)} %bitcast.13, f32[3,16,16,128]{3,2,1,0:T(8,128)} %bitcast.15, f32[16,16,128]{2,1,0:T(8,128)} %bitcast.19, ...), custom_call_target="tpu_custom_call" | custom-call | tf_op jit(solution)/shard_map/pack/pallas_call | solution.py:483
  4.5 102.0 %route.1 = (f32[128,128]{1,0:T(8,128)}, f32[128,128]{1,0:T(8,128)}, f32[16,128]{1,0:T(8,128)}, f32[16,128]{1,0:T(8,128)}) custom-call(f32[128,128]{1,0:T(8,128)} %get-tuple-element.17.first_row, f32[128,128]{1,0:T(8,128)} %get-tuple-element.18.last_row, f32[16,128]{1,0:T(8,128)} %get-tuple-element.19.left_col, f32[16,128]{1,0:T(8,128)} %get-tuple-element.20.right_col, ...), custom_call_target="tpu_custom_call" | custom-call | tf_op jit(solution)/shard_map/route/pallas_call | solution.py:498
  106.5 3.7 %step.1 = (f32[16,16,128]{2,1,0:T(8,128)}, f32[3,16,16,128]{3,2,1,0:T(8,128)}, f32[3,16,16,128]{3,2,1,0:T(8,128)}, f32[16,16,128]{2,1,0:T(8,128)}) custom-call(f32[16,16,128]{2,1,0:T(8,128)} %bitcast.18, f32[3,16,16,128]{3,2,1,0:T(8,128)} %bitcast.14, f32[3,16,16,128]{3,2,1,0:T(8,128)} %bitcast.16, f32[16,16,128]{2,1,0:T(8,128)} %bitcast.20, ...), custom_call_target="tpu_custom_call" | custom-call | tf_op jit(solution)/shard_map/step/pallas_call | solution.py:524

commit v2 on v1

--- a/solution.py
+++ b/solution.py
@@ -48,7 +48,7 @@
     return lax.broadcasted_iota(jnp.int32, shape, dim)
 
 
-def pack_kernel(
+def pack(
     dens, vel, mag, pres, row_in, col_in, weight_in, turn_in, dest_in,
     first_row, last_row, left_col, right_col, donors, ints, floats,
 ):
@@ -116,7 +116,7 @@
         for r in range(6):
             donors[pl.ds(r, 16, stride=8), :] = slots[16 * r : 16 * r + 16, :]
         where_z = jnp.where(z == 0, f, jnp.where(z == NZ - 1, NF + f, 0))
-        where_f = jnp.where(f == 0, 2 * NF + z - 1, 2 * NF + NZ - 2 + z - 1)
+        where_f = 2 * NF + 2 * (z - 1) + jnp.where(f == 0, 0, 1)
         source = jnp.where((z == 0) | (z == NZ - 1), where_z, where_f)
         base = 8 * lax.rem(source, 16)
         slot = iota((16, CP), 1)
@@ -131,10 +131,12 @@
 
 
 def route_kernel(
-    first_row, last_row, left_col, right_col, donors,
+    dens, vel, mag, pres, row_in, col_in, weight_in, turn_in, dest_in,
     out_top, out_bottom, out_left, out_right,
+    first_row, last_row, left_col, right_col, donors, ints, floats,
     top, bottom, left, right, slots, pieces, dense, inbox, total,
-    halo_send, halo_recv, donor_send, donor_recv, dense_send, dense_recv, column_send,
+    halo_send, halo_recv, donor_send, donor_recv, relay_send, relay_recv,
+    dense_send, dense_recv, column_send,
 ):
     p = lax.axis_index("patch")
     z = lax.axis_index("theta")
@@ -152,6 +154,31 @@
     def greet(device):
         pl.semaphore_signal(barrier, inc=1, device_id=device, device_id_type=MESH)
 
+    @pl.when(is_hub)
+    def _():
+        @pl.loop(1, NZ)
+        def _(off):
+            greet((p, lax.rem(z + off, NZ), f))
+
+        @pl.loop(1, NF)
+        def _(off):
+            greet((p, z, lax.rem(f + off, NF)))
+
+    @pl.when(on_row)
+    def _():
+        @pl.loop(0, NF)
+        def _(j):
+            greet((1 - p, z, j))
+
+    @pl.when(jnp.logical_not(on_row))
+    def _():
+        greet((1 - p, z, 0))
+        greet((1 - p, z, NF - 1))
+
+    @pl.when(on_column)
+    def _():
+        greet((p, HUBS[2] + 16 * half, z - 16 * half))
+
     for has, device in (
         (z > 0, (p, z - 1, f)),
         (z < NZ - 1, (p, z + 1, f)),
@@ -160,25 +187,10 @@
     ):
         pl.when(has)(functools.partial(greet, device))
 
-    @pl.when(is_hub)
-    def _():
-        @pl.loop(0, NF)
-        def _(j):
-            greet((1 - p, 0, j))
-            greet((1 - p, NZ - 1, j))
-
-        @pl.loop(1, NZ - 1)
-        def _(j):
-            greet((1 - p, j, 0))
-            greet((1 - p, j, NF - 1))
-
-        @pl.loop(1, NF)
-        def _(off):
-            greet((p, z, lax.rem(f + off, NF)))
-
-    @pl.when(on_column)
-    def _():
-        greet((p, HUBS[2] + 16 * half, z - 16 * half))
+    pack(
+        dens, vel, mag, pres, row_in, col_in, weight_in, turn_in, dest_in,
+        first_row, last_row, left_col, right_col, donors, ints, floats,
+    )
 
     @pl.when(is_hub)
     def _():
@@ -189,9 +201,9 @@
         + jnp.where(z < NZ - 1, 1, 0)
         + jnp.where(f > 0, 1, 0)
         + jnp.where(f < NF - 1, 1, 0)
-        + jnp.where(is_hub, NF - 1, 0)
+        + jnp.where(is_hub, NF - 1 + 3, 4)
         + jnp.where(column_hub, 2, 0)
-        + jnp.where(is_source, 4 * NF, 0)
+        + jnp.where(is_source, NF, 0)
     )
     pl.semaphore_wait(barrier, peers)
 
@@ -214,29 +226,22 @@
     sends_to = (z < NZ - 1, z > 0, f < NF - 1, f > 0)
     hears_from = (z > 0, z < NZ - 1, f > 0, f < NF - 1)
 
-    source = jnp.where(
-        z == 0,
-        f,
-        jnp.where(z == NZ - 1, NF + f, jnp.where(f == 0, 2 * NF + z - 1, 2 * NF + NZ - 3 + z)),
-    )
-
-    def donor_copy(hub, plane, j):
-        return pltpu.make_async_remote_copy(
-            src_ref=donors.at[pl.ds(pl.multiple_of(8 * j, 8), 8)],
-            dst_ref=slots.at[pl.ds(pl.multiple_of(8 * source, 8), 8)],
-            send_sem=donor_send.at[hub],
-            recv_sem=donor_recv,
-            device_id=(1 - p, plane, j),
-            device_id_type=MESH,
-        )
+    plane_low = jnp.where(z == 0, 0, jnp.where(z == NZ - 1, NF, 2 * NF + 2 * (z - 1)))
+    source = plane_low + jnp.where(on_row, f, jnp.where(f == 0, 0, 1))
 
     @pl.when(is_source)
     def _():
         @pl.loop(0, NF)
         def _(off):
             j = lax.rem(f + off, NF)
-            for hub, plane in enumerate(HUBS):
-                donor_copy(hub, plane, j).start()
+            pltpu.make_async_remote_copy(
+                src_ref=donors.at[pl.ds(pl.multiple_of(8 * j, 8), 8)],
+                dst_ref=slots.at[pl.ds(pl.multiple_of(8 * source, 8), 8)],
+                send_sem=donor_send,
+                recv_sem=donor_recv,
+                device_id=(1 - p, z, j),
+                device_id_type=MESH,
+            ).start()
 
     for which in range(4):
 
@@ -246,6 +251,28 @@
 
     def whole_wait(ref, sem):
         return pltpu.make_async_copy(ref, ref, sem).wait()
+
+    def relay(tiles, hub):
+        rows = slots.at[pl.ds(pl.multiple_of(8 * plane_low, 8), 8 * tiles)]
+        return pltpu.make_async_remote_copy(
+            src_ref=rows,
+            dst_ref=rows,
+            send_sem=relay_send.at[hub],
+            recv_sem=relay_recv,
+            device_id=(p, HUBS[hub], f),
+            device_id_type=MESH,
+        )
+
+    for here, tiles in ((on_row, NF), (jnp.logical_not(on_row), 2)):
+
+        @pl.when(here)
+        def _():
+            whole_wait(slots.at[pl.ds(0, 8 * tiles)], donor_recv)
+            for hub in range(4):
+
+                @pl.when(z != HUBS[hub])
+                def _():
+                    relay(tiles, hub).start()
 
     def split_slots():
         value = slots[...]
@@ -290,7 +317,7 @@
 
     @pl.when(on_row)
     def _():
-        whole_wait(slots.at[pl.ds(0, 8 * SOURCES)], donor_recv)
+        whole_wait(slots.at[pl.ds(0, 8 * (SOURCES - NF))], relay_recv)
         ids = split_slots()
         first = 1 + jnp.where(z == 0, 0, NPH)
 
@@ -317,7 +344,7 @@
 
     @pl.when(column_hub)
     def _():
-        whole_wait(slots.at[pl.ds(0, 8 * SOURCES)], donor_recv)
+        whole_wait(slots.at[pl.ds(0, 8 * (SOURCES - 2))], relay_recv)
         ids = split_slots()
         side = lax.rem(point, 32) // 16
         first = 1 + 2 * NPH + NTH * side + lax.rem(point, 16) + CT * (hub_low + point // 32)
@@ -371,8 +398,14 @@
 
     @pl.when(is_source)
     def _():
+        whole_wait(donors, donor_send)
+
+    for here, tiles in ((on_row, NF), (jnp.logical_not(on_row), 2)):
         for hub in range(4):
-            whole_wait(donors, donor_send.at[hub])
+
+            @pl.when(here & (z != HUBS[hub]))
+            def _():
+                relay(tiles, hub).wait_send()
 
 
 def step_kernel(
@@ -480,27 +513,19 @@
     density, velocity, magnetic, pressure, send_row, send_col, send_weight, send_turn, send_dest
 ):
     fields = (density[0], velocity[0], magnetic[0], pressure[0])
-    packed = pl.pallas_call(
-        pack_kernel,
-        out_shape=(shape(CH, CP), shape(CH, CP), shape(CT, CP), shape(CT, CP), shape(CP, CP)),
-        in_specs=[VMEM] * 9,
-        out_specs=(VMEM,) * 5,
-        scratch_shapes=[pltpu.VMEM((8, CP), jnp.int32), pltpu.VMEM((8, CP), F32)],
-        name="pack",
-    )(
-        *fields,
-        send_row.reshape(1, SEND),
-        send_col.reshape(1, SEND),
-        send_weight.reshape(2, SEND),
-        send_turn.reshape(1, SEND),
-        send_dest.reshape(1, SEND),
-    )
     halos = pl.pallas_call(
         route_kernel,
         out_shape=(shape(CH, CP), shape(CH, CP), shape(CT, CP), shape(CT, CP)),
-        in_specs=[VMEM] * 5,
+        in_specs=[VMEM] * 9,
         out_specs=(VMEM,) * 4,
         scratch_shapes=[
+            pltpu.VMEM((CH, CP), F32),
+            pltpu.VMEM((CH, CP), F32),
+            pltpu.VMEM((CT, CP), F32),
+            pltpu.VMEM((CT, CP), F32),
+            pltpu.VMEM((CP, CP), F32),
+            pltpu.VMEM((8, CP), jnp.int32),
+            pltpu.VMEM((8, CP), F32),
             pltpu.VMEM((CH, CP), F32),
             pltpu.VMEM((CH, CP), F32),
             pltpu.VMEM((CT, CP), F32),
@@ -512,6 +537,8 @@
             pltpu.VMEM((32, CP), F32),
             pltpu.SemaphoreType.DMA((4,)),
             pltpu.SemaphoreType.DMA((4,)),
+            pltpu.SemaphoreType.DMA,
+            pltpu.SemaphoreType.DMA,
             pltpu.SemaphoreType.DMA((4,)),
             pltpu.SemaphoreType.DMA,
             pltpu.SemaphoreType.DMA,
@@ -520,7 +547,14 @@
         ],
         compiler_params=pltpu.CompilerParams(collective_id=0, has_side_effects=True),
         name="route",
-    )(*packed)
+    )(
+        *fields,
+        send_row.reshape(1, SEND),
+        send_col.reshape(1, SEND),
+        send_weight.reshape(2, SEND),
+        send_turn.reshape(1, SEND),
+        send_dest.reshape(1, SEND),
+    )
     new_density, new_flow, new_magnet, new_press = pl.pallas_call(
         functools.partial(step_kernel, grid_constants(NTH, NPH)),
         out_shape=(shape(NR, CT, CP), shape(3, NR, CT, CP), shape(3, NR, CT, CP), shape(NR, CT, CP)),

time: 111 us -> 68.5 us (0.62)
  the two profiles are of different devices: /device:TPU:1 before, /device:TPU:25 now
where the time goes in v2:
time: 68.5 us; the launch traced here: 68.3 us
  Pallas kernels  67.7 us (99%)
    pallas_call x1, Pallas kernels, body(): pl.pallas_call(route_kernel, out_shape=(shape(CH, CP), shape(CH, CP), sha...  63.9 us
    pallas_call x1, Pallas kernels, body(): pl.pallas_call(functools.partial(step_kernel, grid_constants(NTH, NPH)),...  3.72 us

profile of v2, /device:TPU:25, one launch (start us, length us, event | category | flops | bytes accessed | tf_op | source)
XLA Modules:
  0.0 68.3 jit_solution(13799587355884217676)
XLA Ops:
  0.6 63.9 %route.1 = (f32[128,128]{1,0:T(8,128)}, f32[128,128]{1,0:T(8,128)}, f32[16,128]{1,0:T(8,128)}, f32[16,128]{1,0:T(8,128)}) custom-call(f32[16,16,128]{2,1,0:T(8,128)} %bitcast.17, f32[3,16,16,128]{3,2,1,0:T(8,128)} %bitcast.13, f32[3,16,16,128]{3,2,1,0:T(8,128)} %bitcast.15, f32[16,16,128]{2,1,0:T(8,128)} %bitcast.19, s32[1,96]{1,0:T(1,128)} %bitcast.22, ...), custom_call_target="tpu_custom_call" | custom-call | tf_op jit(solution)/shard_map/route/pallas_call | solution.py:516
  64.6 3.7 %step.1 = (f32[16,16,128]{2,1,0:T(8,128)}, f32[3,16,16,128]{3,2,1,0:T(8,128)}, f32[3,16,16,128]{3,2,1,0:T(8,128)}, f32[16,16,128]{2,1,0:T(8,128)}) custom-call(f32[16,16,128]{2,1,0:T(8,128)} %bitcast.18, f32[3,16,16,128]{3,2,1,0:T(8,128)} %bitcast.14, f32[3,16,16,128]{3,2,1,0:T(8,128)} %bitcast.16, f32[16,16,128]{2,1,0:T(8,128)} %bitcast.20, ...), custom_call_target="tpu_custom_call" | custom-call | tf_op jit(solution)/shard_map/step/pallas_call | solution.py:558

commit v3 on v2

--- a/solution.py
+++ b/solution.py
@@ -23,7 +23,12 @@
 NPH, NTH = CP * NF, CT * NZ
 SEND = 96
 CH = 8 * NR
-HUBS = (0, NZ - 1, 8, 24)
+HUBS = (0, 1, 2, 20)
+TOP_ROWS = (80, 48)
+STEPS = (
+    (2, 2), (2, 1), (1, 2), (2, 3), (3, 2), (1, 1), (3, 3), (1, 3), (3, 1),
+    (2, 0), (0, 2), (1, 0), (0, 1), (3, 0), (0, 3),
+)
 SOURCES = 2 * NF + 2 * (NZ - 2)
 SLOT_ROWS = 96 * 8
 
@@ -48,13 +53,7 @@
     return lax.broadcasted_iota(jnp.int32, shape, dim)
 
 
-def pack(
-    dens, vel, mag, pres, row_in, col_in, weight_in, turn_in, dest_in,
-    first_row, last_row, left_col, right_col, donors, ints, floats,
-):
-    z = lax.axis_index("theta")
-    f = lax.axis_index("phi")
-    comps = components(dens, vel, mag, pres)
+def pack(comps, first_row, last_row, left_col, right_col):
     for c in range(8):
         first_row[c * NR : (c + 1) * NR, :] = comps[c][:, 0, :]
         last_row[c * NR : (c + 1) * NR, :] = comps[c][:, CT - 1, :]
@@ -71,72 +70,69 @@
     left_col[...] = low
     right_col[...] = high
 
-    @pl.when((z == 0) | (z == NZ - 1) | (f == 0) | (f == NF - 1))
-    def _():
-        ints[...] = jnp.zeros_like(ints)
-        floats[...] = jnp.zeros_like(floats)
-        ints[0:1, 0:SEND] = row_in[...]
-        ints[1:2, 0:SEND] = col_in[...]
-        ints[2:3, 0:SEND] = jnp.where(dest_in[...] < 2 * (NPH + NTH), dest_in[...] + 1, 0)
-        floats[0:2, 0:SEND] = weight_in[...]
-        floats[2:3, 0:SEND] = turn_in[...]
-        row, col, dest = ints[0:1, :], ints[1:2, :], ints[2:3, :]
-        weight_row, weight_col, turn = floats[0:1, :], floats[1:2, :], floats[2:3, :]
-        cell = iota((CP, CP), 0)
-        col_mix = jnp.where(cell == col, 1.0 - weight_col, 0.0) + jnp.where(
-            cell == col + 1, weight_col, 0.0
-        )
-        level = iota((CT, CP), 0)
-        row_mix = jnp.where(level == row, 1.0 - weight_row, 0.0) + jnp.where(
-            level == row + 1, weight_row, 0.0
-        )
-        value = jnp.zeros((CH, CP), F32)
-        for i in range(CT):
-            line = jnp.concatenate([comps[c][:, i, :] for c in range(8)], axis=0)
-            mixed = jnp.dot(
-                line, col_mix, preferred_element_type=F32, precision=lax.Precision.HIGHEST
-            )
-            value = value + row_mix[i : i + 1, :] * mixed
-        cos_t, sin_t = jnp.cos(turn), jnp.sin(turn)
-        part = [value[c * NR : (c + 1) * NR, :] for c in range(8)]
-        turned = jnp.concatenate(
-            [
-                part[0],
-                part[1],
-                cos_t * part[2] + sin_t * part[3],
-                cos_t * part[3] - sin_t * part[2],
-                part[4],
-                cos_t * part[5] + sin_t * part[6],
-                cos_t * part[6] - sin_t * part[5],
-                part[7],
-            ],
-            axis=0,
-        )
-        slots = turned.T
-        for r in range(6):
-            donors[pl.ds(r, 16, stride=8), :] = slots[16 * r : 16 * r + 16, :]
-        where_z = jnp.where(z == 0, f, jnp.where(z == NZ - 1, NF + f, 0))
-        where_f = 2 * NF + 2 * (z - 1) + jnp.where(f == 0, 0, 1)
-        source = jnp.where((z == 0) | (z == NZ - 1), where_z, where_f)
-        base = 8 * lax.rem(source, 16)
-        slot = iota((16, CP), 1)
-        group = iota((16, CP), 0)
-        named = jnp.where(lax.rem(slot, 16) == group, dest.astype(F32), 0.0)
-        slot_down = iota((CP, CP), 0)
-        placed = jnp.where(iota((CP, CP), 1) == base + slot_down // 16, 1.0, 0.0)
-        donors[pl.ds(6, 16, stride=8), :] = jnp.dot(
-            named, placed, preferred_element_type=F32, precision=lax.Precision.HIGHEST
-        )
-        donors[pl.ds(7, 16, stride=8), :] = jnp.zeros((16, CP), F32)
+
+def find_donors(source, comps, row_in, col_in, weight_in, turn_in, dest_in, donors, ints, floats):
+    ints[...] = jnp.zeros_like(ints)
+    floats[...] = jnp.zeros_like(floats)
+    ints[0:1, 0:SEND] = row_in[...]
+    ints[1:2, 0:SEND] = col_in[...]
+    ints[2:3, 0:SEND] = jnp.where(dest_in[...] < 2 * (NPH + NTH), dest_in[...] + 1, 0)
+    floats[0:2, 0:SEND] = weight_in[...]
+    floats[2:3, 0:SEND] = turn_in[...]
+    row, col, dest = ints[0:1, :], ints[1:2, :], ints[2:3, :]
+    weight_row, weight_col, turn = floats[0:1, :], floats[1:2, :], floats[2:3, :]
+    cell = iota((CP, CP), 0)
+    col_mix = jnp.where(cell == col, 1.0 - weight_col, 0.0) + jnp.where(
+        cell == col + 1, weight_col, 0.0
+    )
+    level = iota((CT, CP), 0)
+    row_mix = jnp.where(level == row, 1.0 - weight_row, 0.0) + jnp.where(
+        level == row + 1, weight_row, 0.0
+    )
+    value = jnp.zeros((CH, CP), F32)
+    for i in range(CT):
+        line = jnp.concatenate([comps[c][:, i, :] for c in range(8)], axis=0)
+        mixed = jnp.dot(
+            line, col_mix, preferred_element_type=F32, precision=lax.Precision.HIGHEST
+        )
+        value = value + row_mix[i : i + 1, :] * mixed
+    cos_t, sin_t = jnp.cos(turn), jnp.sin(turn)
+    part = [value[c * NR : (c + 1) * NR, :] for c in range(8)]
+    turned = jnp.concatenate(
+        [
+            part[0],
+            part[1],
+            cos_t * part[2] + sin_t * part[3],
+            cos_t * part[3] - sin_t * part[2],
+            part[4],
+            cos_t * part[5] + sin_t * part[6],
+            cos_t * part[6] - sin_t * part[5],
+            part[7],
+        ],
+        axis=0,
+    )
+    slots = turned.T
+    for r in range(6):
+        donors[pl.ds(r, 16, stride=8), :] = slots[16 * r : 16 * r + 16, :]
+    base = 8 * lax.rem(source, 16)
+    slot = iota((16, CP), 1)
+    group = iota((16, CP), 0)
+    named = jnp.where(lax.rem(slot, 16) == group, dest.astype(F32), 0.0)
+    slot_down = iota((CP, CP), 0)
+    placed = jnp.where(iota((CP, CP), 1) == base + slot_down // 16, 1.0, 0.0)
+    donors[pl.ds(6, 16, stride=8), :] = jnp.dot(
+        named, placed, preferred_element_type=F32, precision=lax.Precision.HIGHEST
+    )
+    donors[pl.ds(7, 16, stride=8), :] = jnp.zeros((16, CP), F32)
 
 
 def route_kernel(
     dens, vel, mag, pres, row_in, col_in, weight_in, turn_in, dest_in,
     out_top, out_bottom, out_left, out_right,
     first_row, last_row, left_col, right_col, donors, ints, floats,
-    top, bottom, left, right, slots, pieces, dense, inbox, total,
+    top, bottom, left, right, slots, pieces, dense, inbox, total, handed,
     halo_send, halo_recv, donor_send, donor_recv, relay_send, relay_recv,
-    dense_send, dense_recv, column_send,
+    dense_send, dense_recv, column_send, hand_send, hand_recv, pass_send,
 ):
     p = lax.axis_index("patch")
     z = lax.axis_index("theta")
@@ -145,21 +141,41 @@
     on_column = (f == 0) | (f == NF - 1)
     is_source = on_row | on_column
     column_hub = (z == HUBS[2]) | (z == HUBS[3])
-    is_hub = on_row | column_hub
+    direct_hub = (z == HUBS[0]) | (z == HUBS[1]) | column_hub
+    is_hub = direct_hub | (z == NZ - 1)
     half = z // 16
     hub_low = 16 * (z // 16)
 
+    def partner(step):
+        dx = sum(jnp.where(step == i, x, 0) for i, (x, _) in enumerate(STEPS))
+        dy = sum(jnp.where(step == i, y, 0) for i, (_, y) in enumerate(STEPS))
+        return 4 * lax.rem(f // 4 + dx, 4) + lax.rem(lax.rem(f, 4) + dy, 4)
+
     barrier = pltpu.get_barrier_semaphore()
 
     def greet(device):
         pl.semaphore_signal(barrier, inc=1, device_id=device, device_id_type=MESH)
 
-    @pl.when(is_hub)
-    def _():
-        @pl.loop(1, NZ)
+    @pl.when(direct_hub)
+    def _():
+        @pl.loop(0, NZ // 2)
+        def _(off):
+            greet((p, lax.rem(z + NZ // 2 + off, NZ), f))
+
+        @pl.loop(1, NZ // 2)
         def _(off):
             greet((p, lax.rem(z + off, NZ), f))
 
+    @pl.when(z == NZ - 1)
+    def _():
+        greet((p, 0, f))
+
+    @pl.when(z == 0)
+    def _():
+        greet((p, 1, f))
+
+    @pl.when(is_hub)
+    def _():
         @pl.loop(1, NF)
         def _(off):
             greet((p, z, lax.rem(f + off, NF)))
@@ -177,7 +193,7 @@
 
     @pl.when(on_column)
     def _():
-        greet((p, HUBS[2] + 16 * half, z - 16 * half))
+        greet((p, jnp.where(half == 0, HUBS[2], HUBS[3]), z - 16 * half))
 
     for has, device in (
         (z > 0, (p, z - 1, f)),
@@ -187,10 +203,15 @@
     ):
         pl.when(has)(functools.partial(greet, device))
 
-    pack(
-        dens, vel, mag, pres, row_in, col_in, weight_in, turn_in, dest_in,
-        first_row, last_row, left_col, right_col, donors, ints, floats,
-    )
+    plane_low = jnp.where(z == 0, 0, jnp.where(z == NZ - 1, NF, 2 * NF + 2 * (z - 1)))
+    source = plane_low + jnp.where(on_row, f, jnp.where(f == 0, 0, 1))
+    comps = components(dens, vel, mag, pres)
+
+    @pl.when(is_source)
+    def _():
+        find_donors(
+            source, comps, row_in, col_in, weight_in, turn_in, dest_in, donors, ints, floats
+        )
 
     @pl.when(is_hub)
     def _():
@@ -201,8 +222,10 @@
         + jnp.where(z < NZ - 1, 1, 0)
         + jnp.where(f > 0, 1, 0)
         + jnp.where(f < NF - 1, 1, 0)
-        + jnp.where(is_hub, NF - 1 + 3, 4)
+        + jnp.where(direct_hub, 3, 4)
+        + jnp.where(is_hub, NF - 1, 0)
         + jnp.where(column_hub, 2, 0)
+        + jnp.where((z == 0) | (z == 1), 1, 0)
         + jnp.where(is_source, NF, 0)
     )
     pl.semaphore_wait(barrier, peers)
@@ -226,14 +249,11 @@
     sends_to = (z < NZ - 1, z > 0, f < NF - 1, f > 0)
     hears_from = (z > 0, z < NZ - 1, f > 0, f < NF - 1)
 
-    plane_low = jnp.where(z == 0, 0, jnp.where(z == NZ - 1, NF, 2 * NF + 2 * (z - 1)))
-    source = plane_low + jnp.where(on_row, f, jnp.where(f == 0, 0, 1))
-
     @pl.when(is_source)
     def _():
         @pl.loop(0, NF)
-        def _(off):
-            j = lax.rem(f + off, NF)
+        def _(step):
+            j = partner(step)
             pltpu.make_async_remote_copy(
                 src_ref=donors.at[pl.ds(pl.multiple_of(8 * j, 8), 8)],
                 dst_ref=slots.at[pl.ds(pl.multiple_of(8 * source, 8), 8)],
@@ -243,6 +263,7 @@
                 device_id_type=MESH,
             ).start()
 
+    pack(comps, first_row, last_row, left_col, right_col)
     for which in range(4):
 
         @pl.when(sends_to[which])
@@ -315,32 +336,73 @@
 
         return lax.fori_loop(1, NF, step, own)
 
-    @pl.when(on_row)
+    def exchange(rows, first):
+        ids = split_slots()
+        points = iota((rows, 1), 0)
+
+        @pl.loop(0, NF)
+        def _(step):
+            j = partner(step)
+            dense[pl.ds(pl.multiple_of(rows * j, rows), rows), :] = place(
+                ids, first + CP * j + points
+            )
+
+            @pl.when(step > 0)
+            def _():
+                block_copy(rows, partner(step - 1)).start()
+
+        return gather_blocks(rows)
+
+    def exchange_done(rows):
+        whole_wait(dense.at[pl.ds(0, rows * (NF - 1))], dense_send)
+
+    def hand_over():
+        return pltpu.make_async_remote_copy(
+            src_ref=total,
+            dst_ref=handed,
+            send_sem=hand_send,
+            recv_sem=hand_recv,
+            device_id=(p, 0, f),
+            device_id_type=MESH,
+        )
+
+    def pass_on(which):
+        low, count = ((0, NF), (2 * NF, SOURCES - 2 * NF))[which]
+        rows = slots.at[pl.ds(8 * low, 8 * count)]
+        return pltpu.make_async_remote_copy(
+            src_ref=rows,
+            dst_ref=rows,
+            send_sem=pass_send.at[which],
+            recv_sem=relay_recv,
+            device_id=(p, NZ - 1, f),
+            device_id_type=MESH,
+        )
+
+    @pl.when(z == 0)
     def _():
         whole_wait(slots.at[pl.ds(0, 8 * (SOURCES - NF))], relay_recv)
-        ids = split_slots()
-        first = 1 + jnp.where(z == 0, 0, NPH)
-
-        @pl.loop(1, NF + 1)
-        def _(off):
-            j = lax.rem(f + off, NF)
-            dense[pl.ds(pl.multiple_of(CP * j, CP), CP), :] = place(ids, first + CP * j + point)
-
-            @pl.when(off > 1)
-            def _():
-                block_copy(CP, lax.rem(f + off - 1, NF)).start()
-
-        border = gather_blocks(CP).T
-
-        @pl.when(z == 0)
-        def _():
-            top[...] = border
-
-        @pl.when(z == NZ - 1)
-        def _():
-            bottom[...] = border
-
-        whole_wait(dense.at[pl.ds(0, CP * (NF - 1))], dense_send)
+        pass_on(0).start()
+        pass_on(1).start()
+        border = exchange(TOP_ROWS[0], 1)
+        whole_wait(handed, hand_recv)
+        top[...] = jnp.concatenate([border, handed[...]], axis=0).T
+        exchange_done(TOP_ROWS[0])
+        pass_on(0).wait_send()
+        pass_on(1).wait_send()
+
+    @pl.when(z == 1)
+    def _():
+        whole_wait(slots.at[pl.ds(0, 8 * (SOURCES - 2))], relay_recv)
+        total[...] = exchange(TOP_ROWS[1], 1 + TOP_ROWS[0])
+        exchange_done(TOP_ROWS[1])
+        hand_over().start()
+        hand_over().wait_send()
+
+    @pl.when(z == NZ - 1)
+    def _():
+        whole_wait(slots.at[pl.ds(0, 8 * (SOURCES - NF))], relay_recv)
+        bottom[...] = exchange(CP, 1 + NPH).T
+        exchange_done(CP)
 
     @pl.when(column_hub)
     def _():
@@ -353,11 +415,12 @@
         def _(quad):
             dense[pl.ds(pl.multiple_of(CP * quad, CP), CP), :] = place(ids, first + CT * 4 * quad)
 
-        @pl.loop(1, NF)
-        def _(off):
-            block_copy(32, lax.rem(f + off, NF)).start()
-
-        total[...] = gather_blocks(32)
+        @pl.loop(0, NF - 1)
+        def _(step):
+            block_copy(32, partner(step)).start()
+
+        total[0:32, :] = gather_blocks(32)
+        whole_wait(dense.at[pl.ds(0, 32 * (NF - 1))], dense_send)
 
         def forward(side_of, dst):
             return pltpu.make_async_remote_copy(
@@ -372,7 +435,6 @@
         copies = [forward(0, left), forward(1, right)]
         for copy in copies:
             copy.start()
-        whole_wait(dense.at[pl.ds(0, 32 * (NF - 1))], dense_send)
         for copy in copies:
             copy.wait_send()
 
@@ -534,13 +596,17 @@
             pltpu.VMEM((SLOT_ROWS, 3 * CP), BF16),
             pltpu.VMEM((NF * CP, CP), F32),
             pltpu.VMEM((NF * CP, CP), F32),
-            pltpu.VMEM((32, CP), F32),
+            pltpu.VMEM((TOP_ROWS[1], CP), F32),
+            pltpu.VMEM((TOP_ROWS[1], CP), F32),
             pltpu.SemaphoreType.DMA((4,)),
             pltpu.SemaphoreType.DMA((4,)),
             pltpu.SemaphoreType.DMA,
             pltpu.SemaphoreType.DMA,
             pltpu.SemaphoreType.DMA((4,)),
             pltpu.SemaphoreType.DMA,
+            pltpu.SemaphoreType.DMA,
+            pltpu.SemaphoreType.DMA,
+            pltpu.SemaphoreType.DMA((2,)),
             pltpu.SemaphoreType.DMA,
             pltpu.SemaphoreType.DMA,
             pltpu.SemaphoreType.DMA((2,)),

time: 68.5 us -> 61.4 us (0.90)
  the two profiles are of different devices: /device:TPU:25 before, /device:TPU:1 now
where the time goes in v3:
time: 61.4 us; the launch traced here: 61.2 us
  Pallas kernels  60.5 us (99%)
  between operations  0.64 us (1%)
    pallas_call x1, Pallas kernels, body(): pl.pallas_call(route_kernel, out_shape=(shape(CH, CP), shape(CH, CP), sha...  56.8 us
    pallas_call x1, Pallas kernels, body(): pl.pallas_call(functools.partial(step_kernel, grid_constants(NTH, NPH)),...  3.72 us

profile of v3, /device:TPU:1, one launch (start us, length us, event | category | flops | bytes accessed | tf_op | source)
XLA Modules:
  0.0 61.2 jit_solution(14515775846980758224)
XLA Ops:
  0.6 56.8 %route.1 = (f32[128,128]{1,0:T(8,128)}, f32[128,128]{1,0:T(8,128)}, f32[16,128]{1,0:T(8,128)}, f32[16,128]{1,0:T(8,128)}) custom-call(f32[16,16,128]{2,1,0:T(8,128)} %bitcast.17, f32[3,16,16,128]{3,2,1,0:T(8,128)} %bitcast.13, f32[3,16,16,128]{3,2,1,0:T(8,128)} %bitcast.15, f32[16,16,128]{2,1,0:T(8,128)} %bitcast.19, s32[1,96]{1,0:T(1,128)} %bitcast.22, ...), custom_call_target="tpu_custom_call" | custom-call | tf_op jit(solution)/shard_map/route/pallas_call | solution.py:578
  57.4 3.7 %step.1 = (f32[16,16,128]{2,1,0:T(8,128)}, f32[3,16,16,128]{3,2,1,0:T(8,128)}, f32[3,16,16,128]{3,2,1,0:T(8,128)}, f32[16,16,128]{2,1,0:T(8,128)}) custom-call(f32[16,16,128]{2,1,0:T(8,128)} %bitcast.18, f32[3,16,16,128]{3,2,1,0:T(8,128)} %bitcast.14, f32[3,16,16,128]{3,2,1,0:T(8,128)} %bitcast.16, f32[16,16,128]{2,1,0:T(8,128)} %bitcast.20, ...), custom_call_target="tpu_custom_call" | custom-call | tf_op jit(solution)/shard_map/step/pallas_call | solution.py:624

commit v4 on v3

--- a/solution.py
+++ b/solution.py
@@ -23,14 +23,15 @@
 NPH, NTH = CP * NF, CT * NZ
 SEND = 96
 CH = 8 * NR
-HUBS = (0, 1, 2, 20)
-TOP_ROWS = (80, 48)
+LOW, HIGH = 1, 20
+TILE, CARRIED = 16, 12
+GROUPS = NF // 2
 STEPS = (
     (2, 2), (2, 1), (1, 2), (2, 3), (3, 2), (1, 1), (3, 3), (1, 3), (3, 1),
     (2, 0), (0, 2), (1, 0), (0, 1), (3, 0), (0, 3),
 )
 SOURCES = 2 * NF + 2 * (NZ - 2)
-SLOT_ROWS = 96 * 8
+SLOT_ROWS = 96 * 16
 
 
 def grid_constants(total_theta, total_phi):
@@ -112,27 +113,28 @@
         axis=0,
     )
     slots = turned.T
-    for r in range(6):
-        donors[pl.ds(r, 16, stride=8), :] = slots[16 * r : 16 * r + 16, :]
-    base = 8 * lax.rem(source, 16)
-    slot = iota((16, CP), 1)
-    group = iota((16, CP), 0)
-    named = jnp.where(lax.rem(slot, 16) == group, dest.astype(F32), 0.0)
+    for r in range(CARRIED):
+        donors[pl.ds(r, GROUPS, stride=TILE), :] = slots[GROUPS * r : GROUPS * (r + 1), :]
+    base = TILE * lax.rem(source, 8)
+    slot = iota((GROUPS, CP), 1)
+    group = iota((GROUPS, CP), 0)
+    named = jnp.where(lax.rem(slot, GROUPS) == group, dest.astype(F32), 0.0)
     slot_down = iota((CP, CP), 0)
-    placed = jnp.where(iota((CP, CP), 1) == base + slot_down // 16, 1.0, 0.0)
-    donors[pl.ds(6, 16, stride=8), :] = jnp.dot(
+    placed = jnp.where(iota((CP, CP), 1) == base + slot_down // GROUPS, 1.0, 0.0)
+    donors[pl.ds(CARRIED, GROUPS, stride=TILE), :] = jnp.dot(
         named, placed, preferred_element_type=F32, precision=lax.Precision.HIGHEST
     )
-    donors[pl.ds(7, 16, stride=8), :] = jnp.zeros((16, CP), F32)
+    for r in range(CARRIED + 1, TILE):
+        donors[pl.ds(r, GROUPS, stride=TILE), :] = jnp.zeros((GROUPS, CP), F32)
 
 
 def route_kernel(
     dens, vel, mag, pres, row_in, col_in, weight_in, turn_in, dest_in,
     out_top, out_bottom, out_left, out_right,
     first_row, last_row, left_col, right_col, donors, ints, floats,
-    top, bottom, left, right, slots, pieces, dense, inbox, total, handed,
+    top, bottom, left, right, slots, pieces, dense, inbox, total,
     halo_send, halo_recv, donor_send, donor_recv, relay_send, relay_recv,
-    dense_send, dense_recv, column_send, hand_send, hand_recv, pass_send,
+    dense_send, dense_recv, column_send, pass_send,
 ):
     p = lax.axis_index("patch")
     z = lax.axis_index("theta")
@@ -140,11 +142,13 @@
     on_row = (z == 0) | (z == NZ - 1)
     on_column = (f == 0) | (f == NF - 1)
     is_source = on_row | on_column
-    column_hub = (z == HUBS[2]) | (z == HUBS[3])
-    direct_hub = (z == HUBS[0]) | (z == HUBS[1]) | column_hub
-    is_hub = direct_hub | (z == NZ - 1)
+    odd = lax.rem(f // 4 + lax.rem(f, 4), 2)
+    even = odd == 0
+    serves_columns = (z == LOW) | (z == HIGH)
+    row_hub = on_row & even
+    column_hub = serves_columns & (odd == 1)
     half = z // 16
-    hub_low = 16 * (z // 16)
+    hub_low = 16 * half
 
     def partner(step):
         dx = sum(jnp.where(step == i, x, 0) for i, (x, _) in enumerate(STEPS))
@@ -156,7 +160,7 @@
     def greet(device):
         pl.semaphore_signal(barrier, inc=1, device_id=device, device_id_type=MESH)
 
-    @pl.when(direct_hub)
+    @pl.when(((z == 0) & even) | column_hub)
     def _():
         @pl.loop(0, NZ // 2)
         def _(off):
@@ -166,19 +170,22 @@
         def _(off):
             greet((p, lax.rem(z + off, NZ), f))
 
-    @pl.when(z == NZ - 1)
+    @pl.when((z == NZ - 1) & even)
     def _():
         greet((p, 0, f))
 
-    @pl.when(z == 0)
-    def _():
-        greet((p, 1, f))
-
-    @pl.when(is_hub)
-    def _():
-        @pl.loop(1, NF)
-        def _(off):
-            greet((p, z, lax.rem(f + off, NF)))
+    def greet_parity(which):
+        @pl.loop(0, GROUPS)
+        def _(g):
+            turn = lax.rem(g // 2, 2)
+            j = 2 * g + (turn if which == 0 else 1 - turn)
+
+            @pl.when(j != f)
+            def _():
+                greet((p, z, j))
+
+    pl.when(on_row)(functools.partial(greet_parity, 0))
+    pl.when(serves_columns)(functools.partial(greet_parity, 1))
 
     @pl.when(on_row)
     def _():
@@ -193,7 +200,7 @@
 
     @pl.when(on_column)
     def _():
-        greet((p, jnp.where(half == 0, HUBS[2], HUBS[3]), z - 16 * half))
+        greet((p, jnp.where(half == 0, LOW, HIGH), z - 16 * half))
 
     for has, device in (
         (z > 0, (p, z - 1, f)),
@@ -213,19 +220,19 @@
             source, comps, row_in, col_in, weight_in, turn_in, dest_in, donors, ints, floats
         )
 
-    @pl.when(is_hub)
-    def _():
-        slots[8 * SOURCES : SLOT_ROWS, :] = jnp.zeros((SLOT_ROWS - 8 * SOURCES, CP), F32)
+    @pl.when(row_hub | column_hub)
+    def _():
+        slots[TILE * SOURCES : SLOT_ROWS, :] = jnp.zeros((SLOT_ROWS - TILE * SOURCES, CP), F32)
 
     peers = (
         jnp.where(z > 0, 1, 0)
         + jnp.where(z < NZ - 1, 1, 0)
         + jnp.where(f > 0, 1, 0)
         + jnp.where(f < NF - 1, 1, 0)
-        + jnp.where(direct_hub, 3, 4)
-        + jnp.where(is_hub, NF - 1, 0)
-        + jnp.where(column_hub, 2, 0)
-        + jnp.where((z == 0) | (z == 1), 1, 0)
+        + jnp.where(even, jnp.where(z != 0, 1, 0), jnp.where(serves_columns, 1, 2))
+        + jnp.where(row_hub | column_hub, NF - 1, 0)
+        + jnp.where(serves_columns, 2, 0)
+        + jnp.where((z == 0) & even, 1, 0)
         + jnp.where(is_source, NF, 0)
     )
     pl.semaphore_wait(barrier, peers)
@@ -255,8 +262,8 @@
         def _(step):
             j = partner(step)
             pltpu.make_async_remote_copy(
-                src_ref=donors.at[pl.ds(pl.multiple_of(8 * j, 8), 8)],
-                dst_ref=slots.at[pl.ds(pl.multiple_of(8 * source, 8), 8)],
+                src_ref=donors.at[pl.ds(pl.multiple_of(TILE * (j // 2), TILE), TILE)],
+                dst_ref=slots.at[pl.ds(pl.multiple_of(TILE * source, TILE), TILE)],
                 send_sem=donor_send,
                 recv_sem=donor_recv,
                 device_id=(1 - p, z, j),
@@ -273,14 +280,17 @@
     def whole_wait(ref, sem):
         return pltpu.make_async_copy(ref, ref, sem).wait()
 
-    def relay(tiles, hub):
-        rows = slots.at[pl.ds(pl.multiple_of(8 * plane_low, 8), 8 * tiles)]
+    PLANES = (0, LOW, HIGH)
+    goes = (even & (z != 0), (odd == 1) & (z != LOW), (odd == 1) & (z != HIGH))
+
+    def relay(tiles, to):
+        rows = slots.at[pl.ds(pl.multiple_of(TILE * plane_low, TILE), TILE * tiles)]
         return pltpu.make_async_remote_copy(
             src_ref=rows,
             dst_ref=rows,
-            send_sem=relay_send.at[hub],
+            send_sem=relay_send.at[to],
             recv_sem=relay_recv,
-            device_id=(p, HUBS[hub], f),
+            device_id=(p, PLANES[to], f),
             device_id_type=MESH,
         )
 
@@ -288,12 +298,12 @@
 
         @pl.when(here)
         def _():
-            whole_wait(slots.at[pl.ds(0, 8 * tiles)], donor_recv)
-            for hub in range(4):
-
-                @pl.when(z != HUBS[hub])
+            whole_wait(slots.at[pl.ds(0, TILE * tiles)], donor_recv)
+            for to in range(3):
+
+                @pl.when(goes[to])
                 def _():
-                    relay(tiles, hub).start()
+                    relay(tiles, to).start()
 
     def split_slots():
         value = slots[...]
@@ -303,9 +313,9 @@
         pieces[:, 0:CP] = high
         pieces[:, CP : 2 * CP] = mid
         pieces[:, 2 * CP :] = (rest - mid.astype(F32)).astype(BF16)
-        ids = slots[pl.ds(6, 96, stride=8), :]
+        ids = slots[pl.ds(CARRIED, 96, stride=TILE), :]
         return jnp.concatenate(
-            [jnp.sum(ids[16 * g : 16 * g + 16, :], axis=0, keepdims=True) for g in range(6)],
+            [jnp.sum(ids[8 * g : 8 * g + 8, :], axis=0, keepdims=True) for g in range(12)],
             axis=1,
         )
 
@@ -314,61 +324,57 @@
         out = jnp.dot(hits, pieces[...], preferred_element_type=F32)
         return out[:, 0:CP] + out[:, CP : 2 * CP] + out[:, 2 * CP :]
 
-    point = iota((CP, 1), 0)
-
     def block_copy(rows, j):
         return pltpu.make_async_remote_copy(
             src_ref=dense.at[pl.ds(pl.multiple_of(rows * j, rows), rows)],
-            dst_ref=inbox.at[pl.ds(pl.multiple_of(rows * f, rows), rows)],
+            dst_ref=inbox.at[pl.ds(pl.multiple_of(rows * (f // 2), rows), rows)],
             send_sem=dense_send,
             recv_sem=dense_recv,
             device_id=(p, z, j),
             device_id_type=MESH,
         )
 
+    def keep_own(rows):
+        mine = dense[pl.ds(pl.multiple_of(rows * f, rows), rows), :]
+        inbox[pl.ds(pl.multiple_of(rows * (f // 2), rows), rows), :] = mine
+
     def gather_blocks(rows):
-        whole_wait(inbox.at[pl.ds(0, rows * (NF - 1))], dense_recv)
-        own = dense[pl.ds(pl.multiple_of(rows * f, rows), rows), :]
-
-        def step(off, acc):
-            j = lax.rem(f + off, NF)
-            return acc + inbox[pl.ds(pl.multiple_of(rows * j, rows), rows), :]
-
-        return lax.fori_loop(1, NF, step, own)
-
-    def exchange(rows, first):
+        for has, count in ((even, GROUPS - 1), (odd == 1, GROUPS)):
+            if rows != CP:
+                count = 2 * GROUPS - 1 - count
+
+            @pl.when(has)
+            def _():
+                whole_wait(inbox.at[pl.ds(0, rows * count)], dense_recv)
+
+        total = inbox[0:rows, :]
+        for g in range(1, GROUPS):
+            total = total + inbox[rows * g : rows * (g + 1), :]
+        return total
+
+    def exchange(first):
         ids = split_slots()
-        points = iota((rows, 1), 0)
-
-        @pl.loop(0, NF)
+        point = iota((2 * CP, 1), 0)
+
+        @pl.loop(0, GROUPS)
         def _(step):
-            j = partner(step)
-            dense[pl.ds(pl.multiple_of(rows * j, rows), rows), :] = place(
-                ids, first + CP * j + points
-            )
+            one, two = partner(2 * step), partner(2 * step + 1)
+            wanted = first + point + jnp.where(point < CP, CP * one, CP * two - CP)
+            blocks = place(ids, wanted)
+            dense[pl.ds(pl.multiple_of(CP * one, CP), CP), :] = blocks[:CP]
+            dense[pl.ds(pl.multiple_of(CP * two, CP), CP), :] = blocks[CP:]
 
             @pl.when(step > 0)
             def _():
-                block_copy(rows, partner(step - 1)).start()
-
-        return gather_blocks(rows)
-
-    def exchange_done(rows):
-        whole_wait(dense.at[pl.ds(0, rows * (NF - 1))], dense_send)
-
-    def hand_over():
-        return pltpu.make_async_remote_copy(
-            src_ref=total,
-            dst_ref=handed,
-            send_sem=hand_send,
-            recv_sem=hand_recv,
-            device_id=(p, 0, f),
-            device_id_type=MESH,
-        )
+                block_copy(CP, partner(2 * step - 2)).start()
+                block_copy(CP, partner(2 * step - 1)).start()
+
+        keep_own(CP)
+        block_copy(CP, partner(NF - 2)).start()
 
     def pass_on(which):
         low, count = ((0, NF), (2 * NF, SOURCES - 2 * NF))[which]
-        rows = slots.at[pl.ds(8 * low, 8 * count)]
+        rows = slots.at[pl.ds(TILE * low, TILE * count)]
         return pltpu.make_async_remote_copy(
             src_ref=rows,
             dst_ref=rows,
@@ -378,36 +384,40 @@
             device_id_type=MESH,
         )
 
+    def forward(side):
+        return pltpu.make_async_remote_copy(
+            src_ref=total.at[pl.ds(CT * side, CT)],
+            dst_ref=(left, right)[side],
+            send_sem=column_send.at[side],
+            recv_sem=halo_recv.at[2 + side],
+            device_id=(p, hub_low + f, (NF - 1) * side),
+            device_id_type=MESH,
+        )
+
+    @pl.when(row_hub)
+    def _():
+        whole_wait(slots.at[pl.ds(0, TILE * (SOURCES - NF))], relay_recv)
+
+        @pl.when(z == 0)
+        def _():
+            pass_on(0).start()
+            pass_on(1).start()
+
+        exchange(1 + jnp.where(z == 0, 0, NPH))
+
     @pl.when(z == 0)
     def _():
-        whole_wait(slots.at[pl.ds(0, 8 * (SOURCES - NF))], relay_recv)
-        pass_on(0).start()
-        pass_on(1).start()
-        border = exchange(TOP_ROWS[0], 1)
-        whole_wait(handed, hand_recv)
-        top[...] = jnp.concatenate([border, handed[...]], axis=0).T
-        exchange_done(TOP_ROWS[0])
-        pass_on(0).wait_send()
-        pass_on(1).wait_send()
-
-    @pl.when(z == 1)
-    def _():
-        whole_wait(slots.at[pl.ds(0, 8 * (SOURCES - 2))], relay_recv)
-        total[...] = exchange(TOP_ROWS[1], 1 + TOP_ROWS[0])
-        exchange_done(TOP_ROWS[1])
-        hand_over().start()
-        hand_over().wait_send()
+        top[...] = gather_blocks(CP).T
 
     @pl.when(z == NZ - 1)
     def _():
-        whole_wait(slots.at[pl.ds(0, 8 * (SOURCES - NF))], relay_recv)
-        bottom[...] = exchange(CP, 1 + NPH).T
-        exchange_done(CP)
+        bottom[...] = gather_blocks(CP).T
 
     @pl.when(column_hub)
     def _():
-        whole_wait(slots.at[pl.ds(0, 8 * (SOURCES - 2))], relay_recv)
+        whole_wait(slots.at[pl.ds(0, TILE * (SOURCES - 2))], relay_recv)
         ids = split_slots()
+        point = iota((CP, 1), 0)
         side = lax.rem(point, 32) // 16
         first = 1 + 2 * NPH + NTH * side + lax.rem(point, 16) + CT * (hub_low + point // 32)
 
@@ -415,24 +425,16 @@
         def _(quad):
             dense[pl.ds(pl.multiple_of(CP * quad, CP), CP), :] = place(ids, first + CT * 4 * quad)
 
+        keep_own(2 * CT)
+
         @pl.loop(0, NF - 1)
         def _(step):
-            block_copy(32, partner(step)).start()
-
-        total[0:32, :] = gather_blocks(32)
-        whole_wait(dense.at[pl.ds(0, 32 * (NF - 1))], dense_send)
-
-        def forward(side_of, dst):
-            return pltpu.make_async_remote_copy(
-                src_ref=total.at[pl.ds(16 * side_of, 16)],
-                dst_ref=dst,
-                send_sem=column_send.at[side_of],
-                recv_sem=halo_recv.at[2 + side_of],
-                device_id=(p, hub_low + f, (NF - 1) * side_of),
-                device_id_type=MESH,
-            )
-
-        copies = [forward(0, left), forward(1, right)]
+            block_copy(2 * CT, partner(step)).start()
+
+    @pl.when(serves_columns)
+    def _():
+        total[...] = gather_blocks(2 * CT)
+        copies = [forward(0), forward(1)]
         for copy in copies:
             copy.start()
         for copy in copies:
@@ -460,14 +462,27 @@
 
     @pl.when(is_source)
     def _():
-        whole_wait(donors, donor_send)
+        whole_wait(slots.at[pl.ds(0, TILE * NF)], donor_send)
 
     for here, tiles in ((on_row, NF), (jnp.logical_not(on_row), 2)):
-        for hub in range(4):
-
-            @pl.when(here & (z != HUBS[hub]))
+        for to in range(3):
+
+            @pl.when(here & goes[to])
             def _():
-                relay(tiles, hub).wait_send()
+                relay(tiles, to).wait_send()
+
+    @pl.when(row_hub)
+    def _():
+        whole_wait(dense.at[pl.ds(0, CP * (NF - 1))], dense_send)
+
+    @pl.when(column_hub)
+    def _():
+        whole_wait(dense.at[pl.ds(0, 2 * CT * (NF - 1))], dense_send)
+
+    @pl.when((z == 0) & even)
+    def _():
+        pass_on(0).wait_send()
+        pass_on(1).wait_send()
 
 
 def step_kernel(
@@ -595,20 +610,17 @@
             pltpu.VMEM((SLOT_ROWS, CP), F32),
             pltpu.VMEM((SLOT_ROWS, 3 * CP), BF16),
             pltpu.VMEM((NF * CP, CP), F32),
-            pltpu.VMEM((NF * CP, CP), F32),
-            pltpu.VMEM((TOP_ROWS[1], CP), F32),
-            pltpu.VMEM((TOP_ROWS[1], CP), F32),
+            pltpu.VMEM((GROUPS * CP, CP), F32),
+            pltpu.VMEM((2 * CT, CP), F32),
             pltpu.SemaphoreType.DMA((4,)),
             pltpu.SemaphoreType.DMA((4,)),
             pltpu.SemaphoreType.DMA,
             pltpu.SemaphoreType.DMA,
-            pltpu.SemaphoreType.DMA((4,)),
+            pltpu.SemaphoreType.DMA((3,)),
             pltpu.SemaphoreType.DMA,
             pltpu.SemaphoreType.DMA,
             pltpu.SemaphoreType.DMA,
             pltpu.SemaphoreType.DMA((2,)),
-            pltpu.SemaphoreType.DMA,
-            pltpu.SemaphoreType.DMA,
             pltpu.SemaphoreType.DMA((2,)),
         ],
         compiler_params=pltpu.CompilerParams(collective_id=0, has_side_effects=True),

time: 61.4 us -> 60.8 us (level)
  Pallas kernels: 60.5 us -> 59.7 us
    pallas_call x1, Pallas kernels: 56.8 us -> 56 us  [body(): pl.pallas_call(route_kernel, out_shape=(shape(CH, CP), shape(CH, CP), sha...]
where the time goes in v4:
time: 60.8 us; the launch traced here: 60.4 us
  Pallas kernels  59.7 us (98%)
  between operations  0.64 us (1%)
    pallas_call x1, Pallas kernels, body(): pl.pallas_call(route_kernel, out_shape=(shape(CH, CP), shape(CH, CP), sha...  56 us
    pallas_call x1, Pallas kernels, body(): pl.pallas_call(functools.partial(step_kernel, grid_constants(NTH, NPH)),...  3.72 us

profile of v4, /device:TPU:1, one launch (start us, length us, event | category | flops | bytes accessed | tf_op | source)
XLA Modules:
  0.0 60.4 jit_solution(2202761245399434286)
XLA Ops:
  0.6 56.0 %route.1 = (f32[128,128]{1,0:T(8,128)}, f32[128,128]{1,0:T(8,128)}, f32[16,128]{1,0:T(8,128)}, f32[16,128]{1,0:T(8,128)}) custom-call(f32[16,16,128]{2,1,0:T(8,128)} %bitcast.17, f32[3,16,16,128]{3,2,1,0:T(8,128)} %bitcast.13, f32[3,16,16,128]{3,2,1,0:T(8,128)} %bitcast.15, f32[16,16,128]{2,1,0:T(8,128)} %bitcast.19, s32[1,96]{1,0:T(1,128)} %bitcast.22, ...), custom_call_target="tpu_custom_call" | custom-call | tf_op jit(solution)/shard_map/route/pallas_call | solution.py:593
  56.7 3.7 %step.1 = (f32[16,16,128]{2,1,0:T(8,128)}, f32[3,16,16,128]{3,2,1,0:T(8,128)}, f32[3,16,16,128]{3,2,1,0:T(8,128)}, f32[16,16,128]{2,1,0:T(8,128)}) custom-call(f32[16,16,128]{2,1,0:T(8,128)} %bitcast.18, f32[3,16,16,128]{3,2,1,0:T(8,128)} %bitcast.14, f32[3,16,16,128]{3,2,1,0:T(8,128)} %bitcast.16, f32[16,16,128]{2,1,0:T(8,128)} %bitcast.20, ...), custom_call_target="tpu_custom_call" | custom-call | tf_op jit(solution)/shard_map/step/pallas_call | solution.py:636

commit v5 on v4

--- a/solution.py
+++ b/solution.py
@@ -23,7 +23,10 @@
 NPH, NTH = CP * NF, CT * NZ
 SEND = 96
 CH = 8 * NR
-LOW, HIGH = 1, 20
+HIGH = 20
+BLOCK = 80
+EVEN_CHIPS = (0, 2, 5, 7, 8, 10, 13, 15)
+ODD_CHIPS = (1, 3, 4, 6, 9, 11, 12, 14)
 TILE, CARRIED = 16, 12
 GROUPS = NF // 2
 STEPS = (
@@ -144,9 +147,8 @@
     is_source = on_row | on_column
     odd = lax.rem(f // 4 + lax.rem(f, 4), 2)
     even = odd == 0
-    serves_columns = (z == LOW) | (z == HIGH)
-    row_hub = on_row & even
-    column_hub = serves_columns & (odd == 1)
+    column_hub = (z == HIGH) & (odd == 1)
+    at_home = (z == 0) & (f == 0)
     half = z // 16
     hub_low = 16 * half
 
@@ -160,7 +162,7 @@
     def greet(device):
         pl.semaphore_signal(barrier, inc=1, device_id=device, device_id_type=MESH)
 
-    @pl.when(((z == 0) & even) | column_hub)
+    @pl.when((z == 0) | column_hub)
     def _():
         @pl.loop(0, NZ // 2)
         def _(off):
@@ -170,23 +172,26 @@
         def _(off):
             greet((p, lax.rem(z + off, NZ), f))
 
-    @pl.when((z == NZ - 1) & even)
+    @pl.when(z == NZ - 1)
     def _():
         greet((p, 0, f))
 
-    def greet_parity(which):
+    @pl.when(on_row)
+    def _():
+        @pl.loop(1, NF)
+        def _(off):
+            greet((p, z, lax.rem(f + off, NF)))
+
+    @pl.when(z == HIGH)
+    def _():
         @pl.loop(0, GROUPS)
         def _(g):
-            turn = lax.rem(g // 2, 2)
-            j = 2 * g + (turn if which == 0 else 1 - turn)
+            j = 2 * g + 1 - lax.rem(g // 2, 2)
 
             @pl.when(j != f)
             def _():
                 greet((p, z, j))
 
-    pl.when(on_row)(functools.partial(greet_parity, 0))
-    pl.when(serves_columns)(functools.partial(greet_parity, 1))
-
     @pl.when(on_row)
     def _():
         @pl.loop(0, NF)
@@ -198,9 +203,9 @@
         greet((1 - p, z, 0))
         greet((1 - p, z, NF - 1))
 
-    @pl.when(on_column)
-    def _():
-        greet((p, jnp.where(half == 0, LOW, HIGH), z - 16 * half))
+    @pl.when(on_column & jnp.logical_not(at_home))
+    def _():
+        greet((p, HIGH * half, z - 16 * half))
 
     for has, device in (
         (z > 0, (p, z - 1, f)),
@@ -220,7 +225,7 @@
             source, comps, row_in, col_in, weight_in, turn_in, dest_in, donors, ints, floats
         )
 
-    @pl.when(row_hub | column_hub)
+    @pl.when(on_row | column_hub)
     def _():
         slots[TILE * SOURCES : SLOT_ROWS, :] = jnp.zeros((SLOT_ROWS - TILE * SOURCES, CP), F32)
 
@@ -229,10 +234,11 @@
         + jnp.where(z < NZ - 1, 1, 0)
         + jnp.where(f > 0, 1, 0)
         + jnp.where(f < NF - 1, 1, 0)
-        + jnp.where(even, jnp.where(z != 0, 1, 0), jnp.where(serves_columns, 1, 2))
-        + jnp.where(row_hub | column_hub, NF - 1, 0)
-        + jnp.where(serves_columns, 2, 0)
-        + jnp.where((z == 0) & even, 1, 0)
+        + jnp.where(z != 0, 1, 2)
+        + jnp.where((odd == 1) & (z != HIGH), 1, 0)
+        + jnp.where(on_row | column_hub, NF - 1, 0)
+        + jnp.where(z == HIGH, 2, 0)
+        + jnp.where(z == 0, jnp.where(f == 0, 0, 1), 0)
         + jnp.where(is_source, NF, 0)
     )
     pl.semaphore_wait(barrier, peers)
@@ -280,8 +286,8 @@
     def whole_wait(ref, sem):
         return pltpu.make_async_copy(ref, ref, sem).wait()
 
-    PLANES = (0, LOW, HIGH)
-    goes = (even & (z != 0), (odd == 1) & (z != LOW), (odd == 1) & (z != HIGH))
+    PLANES = (0, HIGH)
+    goes = (z != 0, (odd == 1) & (z != HIGH))
 
     def relay(tiles, to):
         rows = slots.at[pl.ds(pl.multiple_of(TILE * plane_low, TILE), TILE * tiles)]
@@ -299,7 +305,7 @@
         @pl.when(here)
         def _():
             whole_wait(slots.at[pl.ds(0, TILE * tiles)], donor_recv)
-            for to in range(3):
+            for to in range(2):
 
                 @pl.when(goes[to])
                 def _():
@@ -324,10 +330,14 @@
         out = jnp.dot(hits, pieces[...], preferred_element_type=F32)
         return out[:, 0:CP] + out[:, CP : 2 * CP] + out[:, 2 * CP :]
 
+    def inbox_of(rows):
+        place_in = rows * (f if rows == BLOCK else f // 2)
+        return inbox.at[pl.ds(pl.multiple_of(place_in, 16), rows)]
+
     def block_copy(rows, j):
         return pltpu.make_async_remote_copy(
             src_ref=dense.at[pl.ds(pl.multiple_of(rows * j, rows), rows)],
-            dst_ref=inbox.at[pl.ds(pl.multiple_of(rows * (f // 2), rows), rows)],
+            dst_ref=inbox_of(rows),
             send_sem=dense_send,
             recv_sem=dense_recv,
             device_id=(p, z, j),
@@ -336,41 +346,42 @@
 
     def keep_own(rows):
         mine = dense[pl.ds(pl.multiple_of(rows * f, rows), rows), :]
-        inbox[pl.ds(pl.multiple_of(rows * (f // 2), rows), rows), :] = mine
-
-    def gather_blocks(rows):
-        for has, count in ((even, GROUPS - 1), (odd == 1, GROUPS)):
-            if rows != CP:
-                count = 2 * GROUPS - 1 - count
-
-            @pl.when(has)
-            def _():
-                whole_wait(inbox.at[pl.ds(0, rows * count)], dense_recv)
-
-        total = inbox[0:rows, :]
-        for g in range(1, GROUPS):
-            total = total + inbox[rows * g : rows * (g + 1), :]
-        return total
-
-    def exchange(first):
+        inbox_of(rows)[...] = mine
+
+    def sum_of(rows, places):
+        out = inbox[rows * places[0] : rows * (places[0] + 1), :]
+        for g in places[1:]:
+            out = out + inbox[rows * g : rows * (g + 1), :]
+        return out
+
+    def exchange():
         ids = split_slots()
-        point = iota((2 * CP, 1), 0)
+        row = iota((2 * BLOCK, 1), 0)
+        second = row >= BLOCK
+        t = jnp.where(second, row - BLOCK, row)
+        first = 1 + jnp.where(z == 0, 0, NPH)
+        after = t - (CP - BLOCK)
+        column = 1 + 2 * NPH + jnp.where(after < CT, after, NTH + after - CT)
 
         @pl.loop(0, GROUPS)
         def _(step):
             one, two = partner(2 * step), partner(2 * step + 1)
-            wanted = first + point + jnp.where(point < CP, CP * one, CP * two - CP)
-            blocks = place(ids, wanted)
-            dense[pl.ds(pl.multiple_of(CP * one, CP), CP), :] = blocks[:CP]
-            dense[pl.ds(pl.multiple_of(CP * two, CP), CP), :] = blocks[CP:]
+            j = jnp.where(second, two, one)
+            in_row = first + CP * j + t
+            last = jnp.where(
+                after < 0, in_row + BLOCK, jnp.where(z == 0, column + CT * j, -1)
+            )
+            blocks = place(ids, jnp.where(even, in_row, last))
+            dense[pl.ds(pl.multiple_of(BLOCK * one, BLOCK), BLOCK), :] = blocks[:BLOCK]
+            dense[pl.ds(pl.multiple_of(BLOCK * two, BLOCK), BLOCK), :] = blocks[BLOCK:]
 
             @pl.when(step > 0)
             def _():
-                block_copy(CP, partner(2 * step - 2)).start()
-                block_copy(CP, partner(2 * step - 1)).start()
-
-        keep_own(CP)
-        block_copy(CP, partner(NF - 2)).start()
+                block_copy(BLOCK, partner(2 * step - 2)).start()
+                block_copy(BLOCK, partner(2 * step - 1)).start()
+
+        keep_own(BLOCK)
+        block_copy(BLOCK, partner(NF - 2)).start()
 
     def pass_on(which):
         low, count = ((0, NF), (2 * NF, SOURCES - 2 * NF))[which]
@@ -394,7 +405,7 @@
             device_id_type=MESH,
         )
 
-    @pl.when(row_hub)
+    @pl.when(on_row)
     def _():
         whole_wait(slots.at[pl.ds(0, TILE * (SOURCES - NF))], relay_recv)
 
@@ -403,15 +414,28 @@
             pass_on(0).start()
             pass_on(1).start()
 
-        exchange(1 + jnp.where(z == 0, 0, NPH))
-
-    @pl.when(z == 0)
-    def _():
-        top[...] = gather_blocks(CP).T
-
-    @pl.when(z == NZ - 1)
-    def _():
-        bottom[...] = gather_blocks(CP).T
+        exchange()
+        whole_wait(inbox.at[pl.ds(0, BLOCK * (NF - 1))], dense_recv)
+        rest = sum_of(BLOCK, ODD_CHIPS)
+        total[...] = rest[CP - BLOCK :]
+        border = jnp.concatenate([sum_of(BLOCK, EVEN_CHIPS), rest[: CP - BLOCK]], axis=0).T
+
+        @pl.when(z == 0)
+        def _():
+            @pl.when(f == 0)
+            def _():
+                left[...] = total[0:CT, :]
+
+            @pl.when(f != 0)
+            def _():
+                forward(0).start()
+
+            forward(1).start()
+            top[...] = border
+
+        @pl.when(z == NZ - 1)
+        def _():
+            bottom[...] = border
 
     @pl.when(column_hub)
     def _():
@@ -431,14 +455,17 @@
         def _(step):
             block_copy(2 * CT, partner(step)).start()
 
-    @pl.when(serves_columns)
-    def _():
-        total[...] = gather_blocks(2 * CT)
-        copies = [forward(0), forward(1)]
-        for copy in copies:
-            copy.start()
-        for copy in copies:
-            copy.wait_send()
+    @pl.when(z == HIGH)
+    def _():
+        for has, count in ((even, GROUPS), (odd == 1, GROUPS - 1)):
+
+            @pl.when(has)
+            def _():
+                whole_wait(inbox.at[pl.ds(0, 2 * CT * count)], dense_recv)
+
+        total[...] = sum_of(2 * CT, tuple(range(GROUPS)))
+        forward(0).start()
+        forward(1).start()
 
     for which, ref in enumerate((top, bottom)):
 
@@ -446,8 +473,11 @@
         def _():
             whole_wait(ref, halo_recv.at[which])
 
-    for which, ref in ((2, left), (3, right)):
-        whole_wait(ref, halo_recv.at[which])
+    @pl.when(jnp.logical_not(at_home))
+    def _():
+        whole_wait(left, halo_recv.at[2])
+
+    whole_wait(right, halo_recv.at[3])
 
     out_top[...] = top[...]
     out_bottom[...] = bottom[...]
@@ -465,21 +495,29 @@
         whole_wait(slots.at[pl.ds(0, TILE * NF)], donor_send)
 
     for here, tiles in ((on_row, NF), (jnp.logical_not(on_row), 2)):
-        for to in range(3):
+        for to in range(2):
 
             @pl.when(here & goes[to])
             def _():
                 relay(tiles, to).wait_send()
 
-    @pl.when(row_hub)
-    def _():
-        whole_wait(dense.at[pl.ds(0, CP * (NF - 1))], dense_send)
+    @pl.when(on_row)
+    def _():
+        whole_wait(dense.at[pl.ds(0, BLOCK * (NF - 1))], dense_send)
 
     @pl.when(column_hub)
     def _():
         whole_wait(dense.at[pl.ds(0, 2 * CT * (NF - 1))], dense_send)
 
-    @pl.when((z == 0) & even)
+    @pl.when(((z == 0) & (f != 0)) | (z == HIGH))
+    def _():
+        forward(0).wait_send()
+
+    @pl.when((z == 0) | (z == HIGH))
+    def _():
+        forward(1).wait_send()
+
+    @pl.when(z == 0)
     def _():
         pass_on(0).wait_send()
         pass_on(1).wait_send()
@@ -610,7 +648,7 @@
             pltpu.VMEM((SLOT_ROWS, CP), F32),
             pltpu.VMEM((SLOT_ROWS, 3 * CP), BF16),
             pltpu.VMEM((NF * CP, CP), F32),
-            pltpu.VMEM((GROUPS * CP, CP), F32),
+            pltpu.VMEM((NF * BLOCK, CP), F32),
             pltpu.VMEM((2 * CT, CP), F32),
             pltpu.SemaphoreType.DMA((4,)),
             pltpu.SemaphoreType.DMA((4,)),

time: 60.8 us -> 60.7 us (level); the launches traced: 60.4 us -> 59.5 us
  Pallas kernels: 59.7 us -> 58.9 us
    pallas_call x1, Pallas kernels: 56 us -> 55.2 us  [body(): pl.pallas_call(route_kernel, out_shape=(shape(CH, CP), shape(CH, CP), sha...]
where the time goes in v5:
time: 60.7 us; the launch traced here: 59.5 us
  Pallas kernels  58.9 us (97%)
  between operations  0.64 us (1%)
    pallas_call x1, Pallas kernels, body(): pl.pallas_call(route_kernel, out_shape=(shape(CH, CP), shape(CH, CP), sha...  55.2 us
    pallas_call x1, Pallas kernels, body(): pl.pallas_call(functools.partial(step_kernel, grid_constants(NTH, NPH)),...  3.72 us

profile of v5, /device:TPU:1, one launch (start us, length us, event | category | flops | bytes accessed | tf_op | source)
XLA Modules:
  0.0 59.5 jit_solution(14641537953836994221)
XLA Ops:
  0.6 55.2 %route.1 = (f32[128,128]{1,0:T(8,128)}, f32[128,128]{1,0:T(8,128)}, f32[16,128]{1,0:T(8,128)}, f32[16,128]{1,0:T(8,128)}) custom-call(f32[16,16,128]{2,1,0:T(8,128)} %bitcast.17, f32[3,16,16,128]{3,2,1,0:T(8,128)} %bitcast.13, f32[3,16,16,128]{3,2,1,0:T(8,128)} %bitcast.15, f32[16,16,128]{2,1,0:T(8,128)} %bitcast.19, s32[1,96]{1,0:T(1,128)} %bitcast.22, ...), custom_call_target="tpu_custom_call" | custom-call | tf_op jit(solution)/shard_map/route/pallas_call | solution.py:631
  55.8 3.7 %step.1 = (f32[16,16,128]{2,1,0:T(8,128)}, f32[3,16,16,128]{3,2,1,0:T(8,128)}, f32[3,16,16,128]{3,2,1,0:T(8,128)}, f32[16,16,128]{2,1,0:T(8,128)}) custom-call(f32[16,16,128]{2,1,0:T(8,128)} %bitcast.18, f32[3,16,16,128]{3,2,1,0:T(8,128)} %bitcast.14, f32[3,16,16,128]{3,2,1,0:T(8,128)} %bitcast.16, f32[16,16,128]{2,1,0:T(8,128)} %bitcast.20, ...), custom_call_target="tpu_custom_call" | custom-call | tf_op jit(solution)/shard_map/step/pallas_call | solution.py:674
